TPU v7x, 32 devices: a whole 2x2x4 slice. The times are simulated.
32 devices in a mesh: ctx: 16 (over z, x, core), fsdp: 2 (over y).
Axes of the slice: x: 2, y: 2, z: 4, core: 2. Of those that a mesh axis runs over, the one named last changes fastest.
Arguments:
- layer_input: bfloat16 [2048, 4096], P('ctx'), may hold values from -8 to 8
- gain: float32 [4096], replicated, may hold values from 0.5 to 1.5
- codes: int32 [4096, 384], P('fsdp'), may hold values from -2147483648 to 2147483646
- column_scale_quantized: int32 [64, 3072], P('fsdp'), may hold values from 0 to 255
- block_second_scale: float32 [64], replicated, may hold values from 0.03 to 0.12
- query_down_map: bfloat16 [4096, 16], replicated, may hold values from -0.09375 to 0.09375
- query_up_map: bfloat16 [16, 2048], P(None, 'fsdp'), may hold values from -0.29882812 to 0.29882812
- token_document: int32 [2048], P('ctx'), may hold values from 0 to 3, as said below
- output_cotangent: bfloat16 [2048, 2048], P('ctx', 'fsdp'), may hold values from -0.059814453 to 0.059814453
Outputs:
- attn: bfloat16 [2048, 2048], P('ctx', 'fsdp')
- grad_a: float32 [4096, 16], replicated
- up_map_gradient: float32 [16, 2048], P(None, 'fsdp')
Inputs may be any that keep to these rules, and one draw needn't show every extreme that they name: token_document never falls along the sequence; each document has 1 to 1536 tokens and one has exactly 1536.
All inputs are finite; a program needn't handle non-finite values.
Results may differ from a plain program's by a relative error of at most 0.028.
Values may be sent and summed in bfloat16 or wider, within the bound.
No kernel may reach another device: no remote copies, remote signals or barrier semaphores. Data moves between devices by JAX's collectives and lax.ppermute only.
A program may use at most 192 MiB of HBM per device.

v0:
```python
import math

import jax
import jax.numpy as jnp
from jax import lax
from jax.sharding import PartitionSpec as P

QUERY_HEADS = 16
KEY_VALUE_HEADS = 4
HEAD_SIZE = 128


NF4_LEVELS = [
    -1.0,
    -0.6961928009986877,
    -0.5250730514526367,
    -0.39491748809814453,
    -0.28444138169288635,
    -0.18477343022823334,
    -0.09105003625154495,
    0.0,
    0.07958029955625534,
    0.16093020141124725,
    0.24611230194568634,
    0.33791524171829224,
    0.44070982933044434,
    0.5626170039176941,
    0.7229568362236023,
    1.0,
]
ADAPTER_SCALE = 2.0
ROPE_BASE = 500000.0


def dequantize(packed, column_scale_quantized, block_second_scale):
    row_count = packed.shape[0]
    pieces = [jnp.bitwise_and(jnp.right_shift(packed, 4 * nibble), 15) for nibble in range(8)]
    unpacked = jnp.stack(pieces, axis=-1).reshape(row_count, packed.shape[1] * 8)
    levels = jnp.zeros(unpacked.shape, jnp.float32)
    for slot_code, level_value in enumerate(NF4_LEVELS):
        levels = levels + jnp.where(
            unpacked == slot_code, jnp.float32(level_value), jnp.float32(0.0)
        )
    absmax = (
        (column_scale_quantized.astype(jnp.float32) + 1.0) / 256.0 * block_second_scale[:, None]
    )
    scaled = levels.reshape(row_count // 64, 64, -1) * absmax[:, None, :]
    return scaled.reshape(row_count, -1).astype(jnp.bfloat16)


def rope_angles(positions):
    freqs = jnp.exp(
        jnp.arange(HEAD_SIZE // 2, dtype=jnp.float32) * (-2.0 * math.log(ROPE_BASE) / HEAD_SIZE)
    )
    angle = positions.astype(jnp.float32)[:, None] * freqs[None, :]
    cosine = jnp.concatenate([jnp.cos(angle), jnp.cos(angle)], axis=-1)
    sine = jnp.concatenate([jnp.sin(angle), jnp.sin(angle)], axis=-1)
    return (cosine, sine)


def apply_rotation(field, rotary_phases):
    cosine, sine = rotary_phases
    half = HEAD_SIZE // 2
    turned = jnp.concatenate([-field[..., half:], field[..., :half]], axis=-1)
    return field * cosine[:, None, :] + turned * sine[:, None, :]


def rotate_back(grads, rotary_phases):
    cosine, sine = rotary_phases
    half = HEAD_SIZE // 2
    scaled = grads * sine[:, None, :]
    turned = jnp.concatenate([-scaled[..., half:], scaled[..., :half]], axis=-1)
    return grads * cosine[:, None, :] - turned


def rms_norm(layer_input, gain):
    wide = layer_input.astype(jnp.float32)
    inverse = lax.rsqrt(jnp.mean(wide * wide, axis=-1, keepdims=True) + 1e-05)
    return (wide * inverse * gain[None, :]).astype(jnp.bfloat16)


def fresh_state(head_count, head_grouped, row_count):
    small = jnp.zeros((head_count, head_grouped, row_count), jnp.float32)
    large = jnp.zeros((head_count, head_grouped, row_count, HEAD_SIZE), jnp.float32)
    return (small - 1e30, small, small, large, large, large)


def on_device(
    layer_input,
    gain,
    codes,
    column_scale_quantized,
    block_second_scale,
    query_down_map,
    query_up_map,
    token_document,
    output_cotangent,
):
    row_count = layer_input.shape[0]
    group_total = lax.axis_size("fsdp")
    member = lax.axis_index("fsdp")
    my_place = lax.axis_index("ctx")
    query_width = query_up_map.shape[1]
    heads_here = query_width // HEAD_SIZE
    key_value_heads = KEY_VALUE_HEADS // group_total
    kv_width = key_value_heads * HEAD_SIZE
    group_columns = column_scale_quantized.shape[1] // group_total
    head_grouped = QUERY_HEADS // KEY_VALUE_HEADS
    soft_scale = 1.0 / math.sqrt(HEAD_SIZE)
    all_codes, all_scales = (
        lax.all_gather(codes, "fsdp", axis=0, tiled=True),
        lax.all_gather(column_scale_quantized, "fsdp", axis=0, tiled=True),
    )
    my_codes = lax.dynamic_slice_in_dim(
        all_codes, member * (group_columns // 8), group_columns // 8, 1
    )
    my_scales = lax.dynamic_slice_in_dim(all_scales, member * group_columns, group_columns, 1)
    weight = dequantize(my_codes, my_scales, block_second_scale)
    input_normalized = rms_norm(layer_input, gain)
    projection_output = jnp.dot(input_normalized, weight, preferred_element_type=jnp.float32)
    rank_reduced = jnp.dot(
        input_normalized, query_down_map, preferred_element_type=jnp.float32
    ).astype(jnp.bfloat16)
    query_complete = projection_output[:, :query_width] + ADAPTER_SCALE * jnp.dot(
        rank_reduced, query_up_map, preferred_element_type=jnp.float32
    )
    positions = my_place * row_count + jnp.arange(row_count, dtype=jnp.int32)
    last_position = my_place * row_count + row_count - 1
    rotary_phases = rope_angles(positions)
    query_rows = apply_rotation(
        query_complete.reshape(row_count, heads_here, HEAD_SIZE), rotary_phases
    ).astype(jnp.bfloat16)
    key_rows = apply_rotation(
        projection_output[:, query_width : query_width + kv_width].reshape(
            row_count, key_value_heads, HEAD_SIZE
        ),
        rotary_phases,
    ).astype(jnp.bfloat16)
    value_rows = (
        projection_output[:, query_width + kv_width :]
        .reshape(row_count, key_value_heads, HEAD_SIZE)
        .astype(jnp.bfloat16)
    )
    query_grouped = query_rows.reshape(row_count, key_value_heads, head_grouped, HEAD_SIZE)
    grouped_gradient = output_cotangent.reshape(row_count, key_value_heads, head_grouped, HEAD_SIZE)
    all_ids = lax.all_gather(token_document, "ctx", axis=0, tiled=True)

    def update(state, query_part, grad_part, key_part, value_part, key_start):
        key_count = key_part.shape[0]
        key_pos = key_start + jnp.arange(key_count, dtype=jnp.int32)
        key_ids = lax.dynamic_slice_in_dim(all_ids, key_start, key_count, 0)
        allowed = (token_document[:, None] == key_ids[None, :]) & (
            key_pos[None, :] <= positions[:, None]
        )

        def work(carry):
            run_max, run_sum, run_dot, run_out, run_grad, run_key = carry
            scores = (
                jnp.einsum(
                    "qhgd,khd->hgqk", query_part, key_part, preferred_element_type=jnp.float32
                )
                * soft_scale
            )
            masked = jnp.where(allowed, scores, -1e30)
            new_max = jnp.maximum(run_max, jnp.max(masked, axis=-1))
            expo = jnp.where(allowed, jnp.exp(masked - new_max[..., None]), 0.0)
            decay = jnp.exp(run_max - new_max)
            grad_dots = jnp.einsum(
                "qhgd,khd->hgqk", grad_part, value_part, preferred_element_type=jnp.float32
            )
            weighted = expo * grad_dots
            expo_low = expo.astype(jnp.bfloat16)
            run_sum = decay * run_sum + jnp.sum(expo, axis=-1)
            run_dot = decay * run_dot + jnp.sum(weighted, axis=-1)
            run_out = decay[..., None] * run_out + jnp.einsum(
                "hgqk,khd->hgqd", expo_low, value_part, preferred_element_type=jnp.float32
            )
            run_key = decay[..., None] * run_key + jnp.einsum(
                "hgqk,khd->hgqd", expo_low, key_part, preferred_element_type=jnp.float32
            )
            run_grad = decay[..., None] * run_grad + jnp.einsum(
                "hgqk,khd->hgqd",
                weighted.astype(jnp.bfloat16),
                key_part,
                preferred_element_type=jnp.float32,
            )
            return (new_max, run_sum, run_dot, run_out, run_grad, run_key)

        def unchanged(carry):
            return carry

        active = key_start <= last_position
        return lax.cond(active, work, unchanged, state)

    start_state = fresh_state(key_value_heads, head_grouped, row_count)
    key_piece = lax.all_gather(key_rows, "ctx", axis=0, tiled=True)
    value_piece = lax.all_gather(value_rows, "ctx", axis=0, tiled=True)
    piece_len = key_piece.shape[0]
    key_block = math.gcd(piece_len, max(row_count, 512))
    block_count = piece_len // key_block

    def inner_block(number, carried):
        offset = number * key_block
        key_part = lax.dynamic_slice_in_dim(key_piece, offset, key_block, 0)
        value_part = lax.dynamic_slice_in_dim(value_piece, offset, key_block, 0)
        return update(carried, query_grouped, grouped_gradient, key_part, value_part, offset)

    state = lax.fori_loop(0, block_count, inner_block, start_state)
    run_max, run_sum, run_dot, run_out, run_grad, run_key = state
    output = run_out / run_sum[..., None]
    attn = jnp.transpose(output, (2, 0, 1, 3)).reshape(row_count, query_width).astype(jnp.bfloat16)
    mean_dot = run_dot / run_sum
    grad_query = soft_scale * (run_grad - mean_dot[..., None] * run_key) / run_sum[..., None]
    grad_query = jnp.transpose(grad_query, (2, 0, 1, 3)).reshape(row_count, heads_here, HEAD_SIZE)
    linear_gradient = (
        rotate_back(grad_query, rotary_phases).reshape(row_count, query_width).astype(jnp.bfloat16)
    )
    local_up_map = ADAPTER_SCALE * jnp.dot(
        rank_reduced.T, linear_gradient, preferred_element_type=jnp.float32
    )
    middle_gradient = (
        ADAPTER_SCALE * jnp.dot(linear_gradient, query_up_map.T, preferred_element_type=jnp.float32)
    ).astype(jnp.bfloat16)
    local_a = jnp.dot(input_normalized.T, middle_gradient, preferred_element_type=jnp.float32)
    up_map_gradient = lax.psum(local_up_map, "ctx")
    grad_a = lax.psum(local_a, ("ctx", "fsdp"))
    return (attn, grad_a, up_map_gradient)


def solution(mesh):
    return jax.shard_map(
        on_device,
        mesh=mesh,
        in_specs=(
            P("ctx", None),
            P(),
            P("fsdp", None),
            P("fsdp", None),
            P(),
            P(),
            P(None, "fsdp"),
            P("ctx"),
            P("ctx", "fsdp"),
        ),
        out_specs=(P("ctx", "fsdp"), P(), P(None, "fsdp")),
        check_vma=False,
    )
```

profile of v0, /device:TPU:0, one launch (start us, length us, event | category | flops | bytes accessed | tf_op | source)
XLA Modules:
  0.0 597.2 jit_solution(3610667669623867392)
XLA Ops:
  7.2 3.6 copy.113
  10.9 0.9 copy-done.7
  11.9 12.8 %all_gather.17 = s32[64,3072]{1,0:T(8,128)S(1)} all-gather(s32[32,3072]{1,0:T(8,128)S(1)} %copy-done.7), channel_id=1, replica_groups=mesh['ctx'=16,'fsdp'=2] {'fsdp'}, dimensions={0}, use_global_device_ids=true | all-gather | bytes 1179648 | tf_op jit(solution)/shard_map/all_gather | solution.py:112
  24.7 11.9 %mul.238 = f32[64,64,1536]{2,1,0:T(8,128)} broadcast(f32[64,1536]{1,0:T(8,128)S(1)} %add_multiply_fusion), dimensions={0,2} | broadcast | bytes 25559040 | tf_op jit(solution)/shard_map/mul | solution.py:47
  36.6 24.8 %copy.121 = f32[4096,1536]{0,1:T(8,128)} copy(f32[4096,1536]{1,0:T(8,128)} %bitcast.119) | data formatting | bytes 50331648 | tf_op jit(solution)/shard_map/mul | solution.py:47
  62.2 31.9 %all-gather.5.cloned.1.call-done = s32[4096,384]{0,1:T(8,128)} async-done(((s32[2048,384]{0,1:T(8,128)}), s32[4096,384]{0,1:T(8,128)}) %all-gather.5.cloned.1.call-update) | async-done | bytes 6291472 | tf_op jit(solution)/shard_map/all_gather | solution.py:111
  94.1 6.2 %shift-right-arithmetic_and_fusion = (s32[4096,192]{0,1:T(8,128)}, s32[4096,192,1]{0,1,2:T(8,128)}, s32[4096,192,1]{0,1,2:T(8,128)S(1)}, s32[4096,192,1]{0,1,2:T...) fusion(s32[4096,384]{0,1:T(8,128)} %all-gather.5.cloned.1.call-, ...), kind=kLoop, calls=%fused_computation.36 | loop fusion | flops 12582912 | bytes 28311556 | tf_op jit(solution)/shard_map/and | solution.py:37
  100.3 6.8 %copy.114 = s32[4096,192,1]{0,2,1:T(1,128)} copy(s32[4096,192,1]{0,1,2:T(8,128)} %get-tuple-element.617) | data formatting | bytes 6291456 | tf_op jit(solution)/shard_map/stack | solution.py:38
  107.1 6.8 %copy.115 = s32[4096,192,1]{0,2,1:T(1,128)} copy(s32[4096,192,1]{0,1,2:T(8,128)} %get-tuple-element.611) | data formatting | bytes 6291456 | tf_op jit(solution)/shard_map/stack | solution.py:38
  113.9 4.9 copy.116
  118.8 5.0 copy.117
  123.8 4.9 copy.118
  128.6 4.9 copy.119
  133.6 5.0 copy.120
  138.5 7.4 %stack.34 = s32[4096,192,1]{0,2,1:T(1,128)} reshape(s32[4096,192]{0,1:T(8,128)} %get-tuple-element.610) | data formatting | bytes 6291456 | tf_op jit(solution)/shard_map/stack | solution.py:38
  145.9 66.3 %stack.35 = s32[4096,192,8]{0,2,1:T(8,128)} concatenate(s32[4096,192,1]{0,2,1:T(1,128)} %copy.114, s32[4096,192,1]{0,2,1:T(1,128)} %copy.115, s32[4096,192,1]{0,2,1:T(1,128)} %copy.116, s32[4096,192,1]{0,2,1:T(1,128)} %copy.117, s32[4096,192,1]{0,2,1:T(1,128)} %copy.118, s32[4096,192,1]{0,2,1:T(1,128)} %copy.119, s32[4096,192,1]{0,2,1:T(1,128)} %copy.120, s32[4096,192,1]{0,2,1:T(1,128)} %stack.34), dimensions={2} | concatenate | bytes 50331648 | tf_op jit(solution)/shard_map/stack | solution.py:38
  212.3 42.3 %fusion.25 = f32[128,1536]{1,0:T(8,128)S(1)} fusion(f32[4096,1536]{0,1:T(8,128)} %copy.121, s32[4096,192,8]{0,2,1:T(8,128)} %stack.35, bf16[128,4096]{1,0:T(8,128)(2,1)S(1)} %copy-done.2, f32[4096]{0:T(1024)S(1)} %copy-done.12, f32[128]{0:T(128)S(1)} %add_rsqrt_fusion), kind=kOutput, calls=%fused_computation.35 | convolution fusion | flops 1902116864 | bytes 52183552 | tf_op jit(solution)/shard_map/dot_general | solution.py:120
  256.6 21.3 %all-gather = s32[16,1,128]{2,1,0:T(1,128)S(1)} all-gather(s32[1,1,128]{2,1,0:T(1,128)S(1)} %bitcast.138), channel_id=1, replica_groups=mesh['ctx'=16,'fsdp'=2] {'ctx'}, dimensions={0}, use_global_device_ids=true | all-gather | bytes 8704 | tf_op jit(solution)/shard_map/all_gather | solution.py:146
  279.9 13.7 %all-gather.7.cloned.1.call-done = bf16[2048,2,128]{2,0,1:T(8,128)(2,1)} async-done(((bf16[128,2,128]{2,0,1:T(8,128)(2,1)}), bf16[2048,2,128]{2,0,1:T(8,128)(2,1)}) %all-gather.7.cloned.1.call-update) | async-done | bytes 1048592 | tf_op jit(solution)/shard_map/all_gather | solution.py:196
  293.5 39.6 %all-gather.9.cloned.1.call-done = bf16[2048,2,128]{2,0,1:T(8,128)(2,1)} async-done(((bf16[128,2,128]{2,0,1:T(8,128)(2,1)}), bf16[2048,2,128]{2,0,1:T(8,128)(2,1)}) %all-gather.9.cloned.1.call-update) | async-done | bytes 1048592 | tf_op jit(solution)/shard_map/all_gather | solution.py:197
  333.3 8.3 %while.24 = (s32[]{:T(128)}, f32[2,4,128]{2,1,0:T(4,128)S(1)}, f32[2,4,128]{2,1,0:T(4,128)S(1)}, f32[2,4,128]{2,1,0:T(4,128)S(1)}, f32[2,4,128,128]{3,2,1,0:T(8,...) while((s32[]{:T(128)}, f32[2,4,128]{2,1,0:T(4,128)S(1)}, ...), condition=%wide.region_7.8_spmd.clone, body=%wide.region_1.7_spmd.clone.sunk | while | flops 685182592 | bytes 22270972 | solution.py:208
  333.6 7.8 %conditional.3 = ((f32[2,4,128]{2,1,0:T(4,128)S(1)}, f32[2,4,128]{2,1,0:T(4,128)S(1)}, f32[2,4,128]{2,1,0:T(4,128)S(1)}, f32[2,4,128,128]{3,2,1,0:T(8,128)S(1)},...) conditional(s32[]{:T(128)} %convert_element_type.124, (f32[2,4,128]{2,1,0:T(4,128)S(1)}, ...), branch_computations={%region_2.2_spmd, %region_3.6_spmd} | conditional | flops 685182592 | bytes 22268054 | solution.py:193
  333.9 1.4 fusion.2
  335.4 1.9 fusion.76
  337.3 0.9 convolution_add_fusion
  339.0 1.9 convolution_add_fusion.2
  342.5 1.0 bitcast_multiply_fusion.2
  344.6 1.2 fusion.32
  346.6 106.7 %all-reduce.5.cloned.1.call-done = f32[16,1024]{1,0:T(8,128)} async-done(((f32[16,1024]{1,0:T(8,128)}), f32[16,1024]{1,0:T(8,128)}) %all-reduce.5.cloned.1.call-update) | async-done | bytes 65552 | tf_op jit(solution)/shard_map/psum | solution.py:225
  453.3 134.0 %all-reduce.3.cloned.1.call-done = f32[4096,16]{0,1:T(8,128)} async-done(((f32[4096,16]{0,1:T(8,128)}), f32[4096,16]{0,1:T(8,128)}) %all-reduce.3.cloned.1.call-update) | async-done | bytes 262160 | tf_op jit(solution)/shard_map/psum | solution.py:226
  587.3 1.7 copy.191
  588.9 1.5 copy.192
  (100 shorter events, 9.2 us)
Async XLA Ops:
  7.2 270.8 %copy-start = (bf16[4096,16]{0,1:T(8,128)(2,1)S(1)}, bf16[4096,16]{0,1:T(8,128)(2,1)}, u32[]{:S(2)}) copy-start(bf16[4096,16]{0,1:T(8,128)(2,1)} %param.18) | copy-start | bytes 393220
  7.2 86.9 %all-gather.5.cloned.1.call-start = ((), (), s32[]{:S(2)}) async-start(), calls=%async_computation | async-start | bytes 9437184 | tf_op jit(solution)/shard_map/all_gather | solution.py:111
  10.9 1.0 copy-start.7
  10.9 13.8 %copy-start.14 = (f32[64]{0:T(128)S(1)}, f32[64]{0:T(128)}, u32[]{:S(2)}) copy-start(f32[64]{0:T(128)} %param.17) | copy-start | bytes 772
  10.9 282.6 %all-gather.7.cloned.1.call-start = ((), (), s32[]{:S(2)}) async-start(), calls=%async_computation.1 | async-start | bytes 1114112 | tf_op jit(solution)/shard_map/all_gather | solution.py:196
  36.6 25.3 %copy-start.2 = (bf16[128,4096]{1,0:T(8,128)(2,1)S(1)}, bf16[128,4096]{1,0:T(8,128)(2,1)}, u32[]{:S(2)}) copy-start(bf16[128,4096]{1,0:T(8,128)(2,1)} %param.13) | copy-start | bytes 3145732
  61.7 38.6 %copy-start.4 = (f32[128,128]{0,1:T(8,128)}, f32[128,128]{0,1:T(8,128)S(1)}, u32[]{:S(2)}) copy-start(f32[128,128]{0,1:T(8,128)S(1)} %get-tuple-element.629) | copy-start | bytes 196612
  61.7 38.6 %copy-start.5 = (f32[128,128]{0,1:T(8,128)}, f32[128,128]{0,1:T(8,128)S(1)}, u32[]{:S(2)}) copy-start(f32[128,128]{0,1:T(8,128)S(1)} %get-tuple-element.628) | copy-start | bytes 196612
  145.9 66.3 %copy-start.12 = (f32[4096]{0:T(1024)S(1)}, f32[4096]{0:T(1024)}, u32[]{:S(2)}) copy-start(f32[4096]{0:T(1024)} %param.14) | copy-start | bytes 49156
  212.2 44.0 %copy-start.8 = (bf16[128,1024]{1,0:T(8,128)(2,1)S(1)}, bf16[128,1024]{1,0:T(8,128)(2,1)}, u32[]{:S(2)}) copy-start(bf16[128,1024]{1,0:T(8,128)(2,1)} %param.21) | copy-start | bytes 786436
  212.3 44.3 %copy-start.11 = (s32[128]{0:T(128)S(1)}, s32[128]{0:T(128)}, u32[]{:S(2)}) copy-start(s32[128]{0:T(128)} %param.20) | copy-start | bytes 1540
  254.5 23.9 %copy-start.9 = (bf16[16,1024]{1,0:T(8,128)(2,1)S(1)}, bf16[16,1024]{1,0:T(8,128)(2,1)}, u32[]{:S(2)}) copy-start(bf16[16,1024]{1,0:T(8,128)(2,1)} %param.19) | copy-start | bytes 98308
  255.4 77.7 %all-gather.9.cloned.1.call-start = ((), (), s32[]{:S(2)}) async-start(), calls=%async_computation.2 | async-start | bytes 1114112 | tf_op jit(solution)/shard_map/all_gather | solution.py:197
  256.2 197.1 %all-reduce.5.cloned.1.call-start = ((), (), s32[]{:S(2)}) async-start(), calls=%async_computation.4 | async-start | bytes 131072 | tf_op jit(solution)/shard_map/psum | solution.py:225
  335.4 1.9 copy-start.1
  342.3 1.3 copy-start.6
  342.3 2.2 copy-start.3
  342.4 2.1 copy-start.10
  342.5 2.1 copy-start.13
  344.5 242.8 %all-reduce.3.cloned.1.call-start = ((), (), s32[]{:S(2)}) async-start(), calls=%async_computation.3 | async-start | bytes 524288 | tf_op jit(solution)/shard_map/psum | solution.py:226
Sparse Core Ops, SparseCore 0:
  11.0 83.0 all-gather.4
  255.5 37.9 all-gather.6
  296.3 36.8 all-gather.8
  344.6 108.6 all-reduce.4
  459.2 128.0 all-reduce.2
where the time goes:
time: 609 us; the launch traced here: 597 us
  waiting for transfers between devices  326 us (54%)
  local copies, waits for them, and re-layouts  160 us (26%)
  matrix products  51.8 us (9%)
  blocking collectives  34.1 us (6%)
  between operations  14.5 us (2%)
  other arithmetic  9.96 us (2%)
    psum x1, waiting for transfers between devices, on_device(): grad_a = lax.psum(local_a, ('ctx', 'fsdp'))  134 us
    another operation x9, local copies, waits for them, and re-layouts, dequantize(): jnp.stack(pieces, axis=-1).reshape(row_count, packed.shape[1] * 8)  112 us
    psum x1, waiting for transfers between devices, on_device(): up_map_gradient = lax.psum(local_up_map, 'ctx')  107 us
    dot_general x1, matrix products, on_device(): jnp.dot(input_normalized, weight, preferred_element_type=jnp.float32)  42.3 us
    all_gather x1, waiting for transfers between devices, on_device(): value_piece = lax.all_gather(value_rows, 'ctx', axis=0, tiled=True)  39.6 us
    mul x2, local copies, waits for them, and re-layouts, dequantize(): scaled = levels.reshape(row_count // 64, 64, -1) * absmax[:, None, :]  36.7 us
    all_gather x1, waiting for transfers between devices, on_device(): lax.all_gather(codes, 'fsdp', axis=0, tiled=True)  31.9 us
    all_gather x1, blocking collectives, on_device(): all_ids = lax.all_gather(token_document, 'ctx', axis=0, tiled=True)  21.3 us
  transfers between devices with their start and end apart: 5, of which 5 were waited for; matrix products, arithmetic and copies ran while one was open for 7% of the time, Pallas kernels for 0%

commit v1 on v0

v1 whole, which is shorter than its diff:
```python
import functools
import math

import jax
import jax.numpy as jnp
from jax import lax
from jax.experimental import pallas as pl
from jax.experimental.pallas import tpu as pltpu
from jax.sharding import PartitionSpec as P

HEAD_SIZE = 128
BLOCK_ROWS = 64
NIBBLES = 8
GROUP = HEAD_SIZE // NIBBLES
DEPTH = 256

NF4_LEVELS = [
    -1.0,
    -0.6961928009986877,
    -0.5250730514526367,
    -0.39491748809814453,
    -0.28444138169288635,
    -0.18477343022823334,
    -0.09105003625154495,
    0.0,
    0.07958029955625534,
    0.16093020141124725,
    0.24611230194568634,
    0.33791524171829224,
    0.44070982933044434,
    0.5626170039176941,
    0.7229568362236023,
    1.0,
]
ADAPTER_SCALE = 2.0
ROPE_BASE = 500000.0
F32 = jnp.float32
BF16 = jnp.bfloat16


def vmem(count):
    return [pl.BlockSpec(memory_space=pltpu.VMEM)] * count


def nt(a, b):
    return lax.dot_general(a, b, (((1,), (1,)), ((), ())), preferred_element_type=F32)


def tn(a, b):
    return lax.dot_general(a, b, (((0,), (0,)), ((), ())), preferred_element_type=F32)


def nn(a, b):
    return jnp.dot(a, b, preferred_element_type=F32)


def feature_permutation():
    place = lax.broadcasted_iota(jnp.int32, (HEAD_SIZE, HEAD_SIZE), 0)
    feature = lax.broadcasted_iota(jnp.int32, (HEAD_SIZE, HEAD_SIZE), 1)
    hit = feature == NIBBLES * (place % GROUP) + place // GROUP
    return jnp.where(hit, 1.0, 0.0).astype(BF16)


def spread_scales(scale_ref, second_ref, member, sub_tiles, out_ref):
    blocks = scale_ref.shape[0]
    width = second_ref.shape[1]
    row = lax.broadcasted_iota(jnp.int32, (blocks, width), 0) + member * blocks
    lane = lax.broadcasted_iota(jnp.int32, (blocks, width), 1)
    second = jnp.sum(jnp.where(row == lane, second_ref[...], 0.0), axis=1, keepdims=True)
    order = feature_permutation()
    turned = []
    for tile in sub_tiles:
        if isinstance(tile, int):
            codes = scale_ref[:, tile * HEAD_SIZE : (tile + 1) * HEAD_SIZE]
        else:
            codes = scale_ref[:, pl.ds(pl.multiple_of(tile * HEAD_SIZE, HEAD_SIZE), HEAD_SIZE)]
        absmax = (codes.astype(F32) + 1.0) / 256.0 * second
        turned.append(nt(order, absmax.astype(BF16)))
    for n in range(NIBBLES):
        column = jnp.concatenate([t[n * GROUP : (n + 1) * GROUP] for t in turned], axis=0)
        out_ref[n] = column.T


def project(words, x_ref, x_start, scales_ref, weight_ref, total_ref, row_count):
    steps = row_count // DEPTH

    def fill(step, slot):
        for part in range(DEPTH // BLOCK_ROWS):
            start = pl.multiple_of(step * DEPTH + part * BLOCK_ROWS, BLOCK_ROWS)
            word = words(start)
            block = step * (DEPTH // BLOCK_ROWS) + part
            for half in range(2):
                code = (lax.shift_right_logical(word, 16) if half else word).astype(jnp.int16)
                for quarter in range(4):
                    n = half * 4 + quarter
                    bits = []
                    for b in range(4):
                        place = 4 * quarter + b
                        if place == 15:
                            bits.append(code < jnp.int16(0))
                        else:
                            bits.append((code & jnp.int16(1 << place)) != jnp.int16(0))
                    level = [
                        jnp.where(bits[3], BF16(NF4_LEVELS[8 + j]), BF16(NF4_LEVELS[j]))
                        for j in range(8)
                    ]
                    level = [jnp.where(bits[2], level[4 + j], level[j]) for j in range(4)]
                    level = [jnp.where(bits[1], level[2 + j], level[j]) for j in range(2)]
                    level = jnp.where(bits[0], level[1], level[0])
                    scale = scales_ref[n, pl.ds(block, 1), :].astype(BF16)
                    weight_ref[
                        slot,
                        part * BLOCK_ROWS : (part + 1) * BLOCK_ROWS,
                        n * HEAD_SIZE : (n + 1) * HEAD_SIZE,
                    ] = level * scale

    def multiply(step, slot):
        start = pl.multiple_of(x_start + step * DEPTH, DEPTH)
        total_ref[...] += nn(x_ref[:, pl.ds(start, DEPTH)], weight_ref[slot])

    total_ref[...] = jnp.zeros_like(total_ref)
    fill(0, 0)

    def body(step, carry):
        multiply(step - 1, (step - 1) % 2)
        fill(step, step % 2)
        return carry

    lax.fori_loop(1, steps, body, 0)
    multiply(steps - 1, (steps - 1) % 2)


def key_value_kernel(
    x_ref,
    gain_ref,
    low_codes_ref,
    high_codes_ref,
    scale_ref,
    second_ref,
    down_ref,
    normed_ref,
    low_rank_ref,
    own_ref,
    send_ref,
    scales_ref,
    weight_ref,
    total_ref,
    turned_ref,
):
    member = lax.axis_index("fsdp")
    row_count = low_codes_ref.shape[0]
    wide = x_ref[...].astype(F32)
    inverse = lax.rsqrt(jnp.mean(wide * wide, axis=-1, keepdims=True) + 1e-05)
    normed_ref[...] = (wide * inverse * gain_ref[...]).astype(BF16)
    low_rank_ref[...] = nt(normed_ref[...], down_ref[...]).astype(BF16)
    spread_scales(scale_ref, second_ref, member, [8, 9, 10, 11, 20, 21, 22, 23], scales_ref)
    lane = lax.broadcasted_iota(jnp.int32, (BLOCK_ROWS, HEAD_SIZE), 1)

    def words(start):
        low = low_codes_ref[pl.ds(start, BLOCK_ROWS), :]
        high = high_codes_ref[pl.ds(start, BLOCK_ROWS), :]
        return jnp.where(lane < HEAD_SIZE // 2, low, high)

    project(words, normed_ref, member * row_count, scales_ref, weight_ref, total_ref, row_count)
    half = HEAD_SIZE // 2
    for n in range(NIBBLES):
        turned_ref[...] = total_ref[:, n * HEAD_SIZE : (n + 1) * HEAD_SIZE].T
        own_ref[n] = turned_ref[pl.ds(pl.multiple_of(member * half, half), half), :]
        other = turned_ref[pl.ds(pl.multiple_of((1 - member) * half, half), half), :]
        send_ref[n] = other.astype(BF16)


def query_kernel(
    first,
    x_ref,
    codes_ref,
    scale_ref,
    second_ref,
    out_ref,
    scales_ref,
    weight_ref,
    total_ref,
):
    member = lax.axis_index("fsdp")
    target = (1 - member) if first else member
    row_count = codes_ref.shape[0]
    tiles = [
        jnp.where(target == 0, k, (16 + k) if k < 4 else (8 + k)) for k in range(NIBBLES)
    ]
    spread_scales(scale_ref, second_ref, member, tiles, scales_ref)
    lane = lax.broadcasted_iota(jnp.int32, (BLOCK_ROWS, HEAD_SIZE), 1)
    is_low = target == 0

    def words(start):
        rows = pl.ds(start, BLOCK_ROWS)
        zero = codes_ref[rows, :HEAD_SIZE]
        low = codes_ref[rows, HEAD_SIZE : 2 * HEAD_SIZE]
        high = codes_ref[rows, 2 * HEAD_SIZE :]
        return jnp.where(is_low, zero, jnp.where(lane < HEAD_SIZE // 2, high, low))

    project(words, x_ref, member * row_count, scales_ref, weight_ref, total_ref, row_count)
    for n in range(NIBBLES):
        out_ref[n] = total_ref[:, n * HEAD_SIZE : (n + 1) * HEAD_SIZE].T.astype(out_ref.dtype)


def rotate_pair(a, b, cosine, sine):
    return a * cosine - b * sine, b * cosine + a * sine


def key_value_finish_kernel(own_ref, got_ref, ids_ref, block_ref, cosine_ref, sine_ref):
    row_count = own_ref.shape[2]
    place = lax.axis_index("ctx")
    half = HEAD_SIZE // 2
    row = lax.broadcasted_iota(jnp.int32, (half, row_count), 0)
    token = lax.broadcasted_iota(jnp.int32, (half, row_count), 1) + place * row_count
    index = NIBBLES * (row % NIBBLES) + row // NIBBLES
    freqs = jnp.exp(index.astype(F32) * (-2.0 * math.log(ROPE_BASE) / HEAD_SIZE))
    angle = token.astype(F32) * freqs
    cosine_ref[...] = jnp.cos(angle)
    sine_ref[...] = jnp.sin(angle)
    order = feature_permutation()
    full = [own_ref[n] + got_ref[n].astype(F32) for n in range(NIBBLES)]
    for head in range(2):
        pieces = []
        for n in range(NIBBLES):
            group = full[n][head * GROUP : (head + 1) * GROUP]
            rows = slice(n * NIBBLES, (n + 1) * NIBBLES)
            pieces.extend(
                rotate_pair(group[:NIBBLES], group[NIBBLES:], cosine_ref[rows], sine_ref[rows])
            )
        keys = jnp.concatenate(pieces, axis=0).T.astype(BF16)
        block_ref[0, head * row_count : (head + 1) * row_count, :] = keys
        values = jnp.concatenate(
            [full[n][(2 + head) * GROUP : (3 + head) * GROUP] for n in range(NIBBLES)], axis=0
        )
        values = nn(values.T.astype(BF16), order).astype(BF16)
        block_ref[0, (2 + head) * row_count : (3 + head) * row_count, :] = values
    ids = jnp.broadcast_to(ids_ref[...].astype(F32), (GROUP, row_count))
    block_ref[0, 4 * row_count :, :] = ids.astype(BF16)


def query_finish_kernel(
    own_ref, got_ref, low_rank_ref, up_ref, cosine_ref, sine_ref, queries_ref, full_ref
):
    member = lax.axis_index("fsdp")
    order = feature_permutation()
    heads = queries_ref.shape[0]
    for n in range(NIBBLES):
        full_ref[n] = own_ref[n] + got_ref[n].astype(F32)
    for head in range(heads):
        up = nt(up_ref[:, head * HEAD_SIZE : (head + 1) * HEAD_SIZE], order).astype(BF16)
        adapter = ADAPTER_SCALE * lax.dot_general(
            up, low_rank_ref[...], (((0,), (1,)), ((), ())), preferred_element_type=F32
        )
        start = pl.multiple_of(((head + member * (heads // 2)) % heads) * GROUP, GROUP)
        pieces = []
        for n in range(NIBBLES):
            group = full_ref[n, pl.ds(start, GROUP), :] + adapter[n * GROUP : (n + 1) * GROUP]
            rows = slice(n * NIBBLES, (n + 1) * NIBBLES)
            pieces.extend(
                rotate_pair(group[:NIBBLES], group[NIBBLES:], cosine_ref[rows], sine_ref[rows])
            )
        queries_ref[head] = jnp.concatenate(pieces, axis=0).T.astype(BF16)


def attention_kernel(
    context,
    queries_ref,
    cotangent_ref,
    own_ref,
    beside_ref,
    core_ref,
    core_beside_ref,
    low_rank_ref,
    normed_ref,
    up_ref,
    cosine_ref,
    sine_ref,
    attn_ref,
    mine_ref,
    other_ref,
    grads_ref,
    top_ref,
    norm_ref,
    dot_ref,
    out_ref,
    grad_ref,
    lin_ref,
):
    place = lax.axis_index("ctx")
    heads, row_count, _ = queries_ref.shape
    grouped = heads // 2
    lists = own_ref.shape[0]
    depth = context.bit_length() - 1
    soft = math.log2(math.e) / math.sqrt(HEAD_SIZE)
    for head in range(heads):
        rows = slice((head % grouped) * row_count, (head % grouped + 1) * row_count)
        grads_ref[head // grouped, rows, :] = cotangent_ref[
            :, head * HEAD_SIZE : (head + 1) * HEAD_SIZE
        ]
    top_ref[...] = jnp.full_like(top_ref, -1e30)
    norm_ref[...] = jnp.zeros_like(norm_ref)
    dot_ref[...] = jnp.zeros_like(dot_ref)
    out_ref[...] = jnp.zeros_like(out_ref)
    grad_ref[...] = jnp.zeros_like(grad_ref)
    square = (row_count, row_count)
    my_ids = own_ref[0, 4 * row_count :, :].astype(F32)[:1]
    row_ids = jnp.broadcast_to(my_ids, square).T
    row_pos = lax.broadcasted_iota(jnp.int32, square, 0) + place * row_count
    lane = lax.broadcasted_iota(jnp.int32, square, 1)
    pieces = (own_ref, beside_ref, core_ref, core_beside_ref)

    def chunk(number, device):
        bias = []
        for piece, flip in zip(pieces, (0, 2, 1, 3)):
            ids = piece[number, 4 * row_count :, :].astype(F32)[:1]
            pos = lane + (device ^ flip) * row_count
            allowed = (row_ids == ids) & (pos <= row_pos)
            bias.append(jnp.where(allowed, 0.0, -1e30))
        bias = jnp.concatenate(bias, axis=1)
        for kv in range(2):
            key_rows = slice(kv * row_count, (kv + 1) * row_count)
            value_rows = slice((2 + kv) * row_count, (3 + kv) * row_count)
            keys = jnp.concatenate([piece[number, key_rows, :] for piece in pieces], axis=0)
            values = jnp.concatenate([piece[number, value_rows, :] for piece in pieces], axis=0)
            both = jnp.concatenate([values, keys], axis=1)
            for g in range(grouped):
                rows = slice(g * row_count, (g + 1) * row_count)
                scores = nt(queries_ref[kv * grouped + g], keys) * soft + bias
                dots = nt(grads_ref[kv, rows, :], values)
                old = top_ref[kv, rows, :]
                new = jnp.maximum(old, jnp.max(scores, axis=1, keepdims=True))
                top_ref[kv, rows, :] = new
                decay = jnp.exp2(old - new)
                expo = jnp.exp2(scores - jnp.concatenate([new] * 4, axis=1))
                weighted = expo * dots
                fold = lambda a: (
                    a[:, :HEAD_SIZE]
                    + a[:, HEAD_SIZE : 2 * HEAD_SIZE]
                    + a[:, 2 * HEAD_SIZE : 3 * HEAD_SIZE]
                    + a[:, 3 * HEAD_SIZE :]
                )
                norm_ref[kv, rows, :] = decay * norm_ref[kv, rows, :] + fold(expo)
                dot_ref[kv, rows, :] = decay * dot_ref[kv, rows, :] + fold(weighted)
                wide = jnp.concatenate([decay, decay], axis=1)
                out_ref[kv, rows, :] = wide * out_ref[kv, rows, :] + nn(expo.astype(BF16), both)
                grad_ref[kv, rows, :] = decay * grad_ref[kv, rows, :] + nn(
                    weighted.astype(BF16), keys
                )

    def body(number, carry):
        flip = 0
        for b in range(depth - 2):
            flip = flip + (((number >> b) & 1) << (depth - 1 - b))
        device = place ^ flip

        @pl.when((device >> 2) <= (place >> 2))
        def _():
            chunk(number, device)

        return carry

    lax.fori_loop(0, lists, body, 0)

    half = HEAD_SIZE // 2
    cosine, sine = [], []
    for n in range(NIBBLES):
        rows = slice(n * NIBBLES, (n + 1) * NIBBLES)
        cosine.extend([cosine_ref[rows]] * 2)
        sine.extend([sine_ref[rows], -sine_ref[rows]])
    cosine = jnp.concatenate(cosine, axis=0).T
    sine = jnp.concatenate(sine, axis=0).T
    low_half = (lax.broadcasted_iota(jnp.int32, square, 1) & NIBBLES) == 0
    order = feature_permutation()
    for head in range(heads):
        kv, g = divmod(head, grouped)
        rows = slice(g * row_count, (g + 1) * row_count)
        columns = slice(head * HEAD_SIZE, (head + 1) * HEAD_SIZE)
        inverse = 1.0 / jnp.sum(norm_ref[kv, rows, :], axis=1, keepdims=True)
        attn_ref[:, columns] = (out_ref[kv, rows, :HEAD_SIZE] * inverse).astype(BF16)
        mean = jnp.sum(dot_ref[kv, rows, :], axis=1, keepdims=True) * inverse
        grad = (grad_ref[kv, rows, :] - mean * out_ref[kv, rows, HEAD_SIZE:]) * (
            inverse * (1.0 / math.sqrt(HEAD_SIZE))
        )
        swapped = jnp.where(
            low_half,
            pltpu.roll(grad, HEAD_SIZE - NIBBLES, 1),
            pltpu.roll(grad, NIBBLES, 1),
        )
        lin = (grad * cosine + swapped * sine).astype(BF16)
        lin_ref[:, columns] = nn(lin, order).astype(BF16)
    middle = (ADAPTER_SCALE * nt(lin_ref[...], up_ref[...])).astype(BF16)
    core = place & 1
    width = normed_ref.shape[1] // 2
    up_width = lin_ref.shape[1] // 2
    mine = pl.ds(pl.multiple_of(core * width, HEAD_SIZE), width)
    other = pl.ds(pl.multiple_of((1 - core) * width, HEAD_SIZE), width)
    mine_ref[:, :width] = tn(middle, normed_ref[:, mine])
    other_ref[:, :width] = tn(middle, normed_ref[:, other]).astype(BF16)
    mine = pl.ds(pl.multiple_of(core * up_width, HEAD_SIZE), up_width)
    other = pl.ds(pl.multiple_of((1 - core) * up_width, HEAD_SIZE), up_width)
    mine_ref[:, width:] = ADAPTER_SCALE * tn(low_rank_ref[...], lin_ref[:, mine])
    other_ref[:, width:] = (ADAPTER_SCALE * tn(low_rank_ref[...], lin_ref[:, other])).astype(BF16)


def cost(flops, size):
    return pl.CostEstimate(flops=int(flops), bytes_accessed=int(size), transcendentals=0)


def on_device(
    context,
    layer_input,
    gain,
    codes,
    column_scale_quantized,
    block_second_scale,
    query_down_map,
    query_up_map,
    token_document,
    output_cotangent,
):
    row_count, width = layer_input.shape
    code_rows, code_width = codes.shape
    rank = query_down_map.shape[1]
    query_width = query_up_map.shape[1]
    heads = query_width // HEAD_SIZE
    half = HEAD_SIZE // 2
    sds = jax.ShapeDtypeStruct

    def flip(array, bit):
        return lax.ppermute(array, "ctx", [(i, i ^ bit) for i in range(context)])

    def swap(array):
        return lax.ppermute(array, "fsdp", [(0, 1), (1, 0)])

    gain_row = gain.reshape(1, width)
    second_row = block_second_scale.reshape(1, -1)
    ids_row = token_document.reshape(1, row_count)
    down_rows = query_down_map.T
    project_scratch = [
        pltpu.VMEM((NIBBLES, code_rows // BLOCK_ROWS, HEAD_SIZE), F32),
        pltpu.VMEM((2, DEPTH, NIBBLES * HEAD_SIZE), BF16),
        pltpu.VMEM((row_count, NIBBLES * HEAD_SIZE), F32),
    ]
    project_cost = cost(1.2e10, code_rows * HEAD_SIZE * 4)
    whole = lambda a: pl.BlockSpec(a.shape, lambda i: (0,) * a.ndim)
    normed, low_rank, kv_own, kv_send = pl.pallas_call(
        key_value_kernel,
        grid=(1,),
        in_specs=[
            whole(layer_input),
            whole(gain_row),
            pl.BlockSpec((code_rows, HEAD_SIZE), lambda i: (0, 1)),
            pl.BlockSpec((code_rows, HEAD_SIZE), lambda i: (0, 2)),
            whole(column_scale_quantized),
            whole(second_row),
            whole(down_rows),
        ],
        out_specs=vmem(4),
        out_shape=[
            sds((row_count, width), BF16),
            sds((row_count, rank), BF16),
            sds((NIBBLES, half, row_count), F32),
            sds((NIBBLES, half, row_count), BF16),
        ],
        scratch_shapes=project_scratch + [pltpu.VMEM((HEAD_SIZE, row_count), F32)],
        cost_estimate=project_cost,
        name="key_value_projection",
    )(
        layer_input,
        gain_row,
        codes,
        codes,
        column_scale_quantized,
        second_row,
        down_rows,
    )
    kv_got = swap(kv_send)

    def query_projection(first, dtype):
        return pl.pallas_call(
            functools.partial(query_kernel, first),
            in_specs=vmem(4),
            out_specs=pl.BlockSpec(memory_space=pltpu.VMEM),
            out_shape=sds((NIBBLES, HEAD_SIZE, row_count), dtype),
            scratch_shapes=project_scratch,
            cost_estimate=project_cost,
            name="query_send" if first else "query_own",
        )(normed, codes, column_scale_quantized, second_row)

    q_send = query_projection(True, BF16)
    block, cosine, sine = pl.pallas_call(
        key_value_finish_kernel,
        in_specs=vmem(3),
        out_specs=vmem(3),
        out_shape=[
            sds((1, 4 * row_count + GROUP, HEAD_SIZE), BF16),
            sds((half, row_count), F32),
            sds((half, row_count), F32),
        ],
        cost_estimate=cost(1e9, 1e6),
        name="key_value_finish",
    )(kv_own, kv_got, ids_row)
    q_got = swap(q_send)
    q_own = query_projection(False, F32)
    queries = pl.pallas_call(
        query_finish_kernel,
        in_specs=vmem(6),
        out_specs=pl.BlockSpec(memory_space=pltpu.VMEM),
        out_shape=sds((heads, row_count, HEAD_SIZE), BF16),
        scratch_shapes=[pltpu.VMEM((NIBBLES, HEAD_SIZE, row_count), F32)],
        cost_estimate=cost(2e9, 1e6),
        name="query_finish",
    )(q_own, q_got, low_rank, query_up_map, cosine, sine)

    bit = context // 2
    while bit > 2:
        block = jnp.concatenate([block, flip(block, bit)], axis=0)
        bit //= 2
    beside = flip(block, 2)
    core = flip(block, 1)
    core_beside = flip(beside, 1)

    total = width // 2 + query_width // 2
    stacked = (2, heads // 2 * row_count, HEAD_SIZE)
    doubled = (2, heads // 2 * row_count, 2 * HEAD_SIZE)
    attn, mine, other = pl.pallas_call(
        functools.partial(attention_kernel, context),
        in_specs=vmem(11),
        out_specs=vmem(3),
        out_shape=[
            sds((row_count, query_width), BF16),
            sds((rank, total), F32),
            sds((rank, total), BF16),
        ],
        scratch_shapes=[
            pltpu.VMEM(stacked, BF16),
            pltpu.VMEM(stacked, F32),
            pltpu.VMEM(stacked, F32),
            pltpu.VMEM(stacked, F32),
            pltpu.VMEM(doubled, F32),
            pltpu.VMEM(stacked, F32),
            pltpu.VMEM((row_count, query_width), BF16),
        ],
        cost_estimate=cost(1e10, 1e6),
        name="attention",
    )(
        queries,
        output_cotangent,
        block,
        beside,
        core,
        core_beside,
        low_rank,
        normed,
        query_up_map,
        cosine,
        sine,
    )

    summed = mine + flip(other, 1).astype(F32)
    bit = 2
    while bit < context:
        summed = summed + flip(summed.astype(BF16), bit).astype(F32)
        bit *= 2
    down = summed[:, : width // 2]
    down = down + swap(down.astype(BF16)).astype(F32)
    packed = jnp.concatenate([down, summed[:, width // 2 :]], axis=1)
    partner = flip(packed, 1)
    low = (lax.axis_index("ctx") & 1) == 0
    first = jnp.where(low, packed, partner)
    second = jnp.where(low, partner, packed)
    grad_a = jnp.concatenate([first[:, : width // 2], second[:, : width // 2]], axis=1).T
    up_map_gradient = jnp.concatenate([first[:, width // 2 :], second[:, width // 2 :]], axis=1)
    return (attn, grad_a, up_map_gradient)


def solution(mesh):
    return jax.shard_map(
        functools.partial(on_device, mesh.shape["ctx"]),
        mesh=mesh,
        in_specs=(
            P("ctx", None),
            P(),
            P("fsdp", None),
            P("fsdp", None),
            P(),
            P(),
            P(None, "fsdp"),
            P("ctx"),
            P("ctx", "fsdp"),
        ),
        out_specs=(P("ctx", "fsdp"), P(), P(None, "fsdp")),
        check_vma=False,
    )
```

time: 609 us -> 106 us (0.17); the launches traced: 597 us -> 106 us
  waiting for transfers between devices: 326 us -> 29.9 us
  local copies, waits for them, and re-layouts: 160 us -> 3.97 us
  matrix products: 51.8 us -> 0 us
  Pallas kernels: 0 us -> 39.1 us
  blocking collectives: 34.1 us -> 0 us
  starting transfers between devices: 0.21 us -> 25.7 us
  between operations: 14.5 us -> 0.77 us
    psum x2 -> x0, waiting for transfers between devices: 241 us -> none  [the longest x1 134 us: on_device(): grad_a = lax.psum(local_a, ('ctx', 'fsdp'))]
    another operation x9 -> x0, local copies, waits for them, and re-layouts: 112 us -> none  [dequantize(): jnp.stack(pieces, axis=-1).reshape(row_count, packed.shape[1] * 8)]
    all_gather x3 -> x0, waiting for transfers between devices: 85.2 us -> none  [the longest x1 39.6 us: on_device(): value_piece = lax.all_gather(value_rows, 'ctx', axis=0, tiled=True)]
    dot_general x10 -> x0, matrix products: 51.8 us -> none  [the longest x1 42.3 us: on_device(): jnp.dot(input_normalized, weight, preferred_element_type=jnp.float32)]
    pallas_call x0 -> x6, Pallas kernels: none -> 39.1 us  [the longest x2 17.9 us: query_projection(): pl.pallas_call(functools.partial(query_kernel, first), in_specs=vmem(4),...]
    mul x2 -> x0, local copies, waits for them, and re-layouts: 36.7 us -> none  [dequantize(): scaled = levels.reshape(row_count // 64, 64, -1) * absmax[:, None, :]]
    all_gather x2 -> x0, blocking collectives: 34.1 us -> none  [the longest x1 21.3 us: on_device(): all_ids = lax.all_gather(token_document, 'ctx', axis=0, tiled=True)]
    ppermute x0 -> x13, waiting for transfers between devices: none -> 29.9 us  [the longest x10 23.3 us: flip(): return lax.ppermute(array, 'ctx', [(i, i ^ bit) for i in range(context)])]
  transfers between devices with their start and end apart: 5 -> 13, of which waited for: 5 -> 10; matrix products, arithmetic and copies ran while one was open for 7% -> 1% of each run, Pallas kernels for 0% -> 19%
where the time goes in v1:
time: 106 us
  Pallas kernels  39.1 us (37%)
  waiting for transfers between devices  29.9 us (28%)
  starting transfers between devices  25.7 us (24%)
  other arithmetic  6.16 us (6%)
  local copies, waits for them, and re-layouts  3.97 us (4%)
    ppermute x10, waiting for transfers between devices, flip(): return lax.ppermute(array, 'ctx', [(i, i ^ bit) for i in range(context)])  23.3 us
    ppermute x10, starting transfers between devices, flip(): return lax.ppermute(array, 'ctx', [(i, i ^ bit) for i in range(context)])  19.8 us
    pallas_call x2, Pallas kernels, query_projection(): pl.pallas_call(functools.partial(query_kernel, first), in_specs=vmem(4),...  17.9 us
    pallas_call x1, Pallas kernels, on_device(): pl.pallas_call(key_value_kernel, grid=(1,), in_specs=[whole(layer_input),...  9.17 us
    pallas_call x1, Pallas kernels, on_device(): pl.pallas_call(functools.partial(attention_kernel, context), in_specs=vme...  7.55 us
    ppermute x3, waiting for transfers between devices, swap(): return lax.ppermute(array, 'fsdp', [(0, 1), (1, 0)])  6.68 us
    ppermute x3, starting transfers between devices, swap(): return lax.ppermute(array, 'fsdp', [(0, 1), (1, 0)])  5.87 us
    unnamed x14, local copies, waits for them, and re-layouts  3.9 us
  transfers between devices with their start and end apart: 13, of which 10 were waited for; matrix products, arithmetic and copies ran while one was open for 1% of the time, Pallas kernels for 19%

profile of v1, /device:TPU:0, one launch (start us, length us, event | category | flops | bytes accessed | tf_op | source)
XLA Modules:
  0.0 105.6 jit_solution(9303569712796168237)
XLA Ops:
  0.6 9.2 %key_value_projection.1 = (bf16[128,4096]{1,0:T(8,128)(2,1)}, bf16[128,16]{1,0:T(8,128)(2,1)}, f32[8,64,128]{2,1,0:T(8,128)}, bf16[8,64,128]{2,1,0:T(8,128)(2,1)}) custom-call(bf16[128,4096]{1,0:T(8,128)(2,1)} %x_ref.1, f32[1,4096]{1,0:T(1,128)} %bitcast.7, s32[2048,384]{1,0:T(8,128)} %codes_ref.3, s32[2048,384]{1,0:T(8,128)} %codes_ref.3, ...), custom_call_target="tpu_custom_call" | custom-call | flops 12000000000 | bytes 1048576 | tf_op jit(solution)/shard_map/key_value_projection/pallas_call | solution.py:447
  9.8 3.0 %collective-permute-start.1 = (bf16[8,64,128]{2,1,0:T(8,128)(2,1)}, bf16[8,64,128]{2,1,0:T(8,128)(2,1)S(1)}, u32[]{:S(2)}, u32[]{:S(2)}) collective-permute-start(bf16[8,64,128]{2,1,0:T(8,128)(2,1)} %get-tuple-element.16), channel_id=1, source_target_pairs={{0,1},{1,0},{2,3},{3,2},{4,5},{5,4},{6,7},{7,6},{8,9},{9,8},{10,11... | collective-permute-start | bytes 393224 | tf_op jit(solution)/shard_map/ppermute | solution.py:434
  12.8 3.7 %collective-permute-done.1.got_ref = bf16[8,64,128]{2,1,0:T(8,128)(2,1)S(1)} collective-permute-done((bf16[8,64,128]{2,1,0:T(8,128)(2,1)}, bf16[8,64,128]{2,1,0:T(8,128)(2,1)S(1)}, u32[]{:S(2)}, u32[]{:S(2)}) %collective-permute-start.1) | collective-permute-done | bytes 131104 | tf_op jit(solution)/shard_map/ppermute | solution.py:434
  17.2 2.0 %key_value_finish.1 = (bf16[1,528,128]{2,1,0:T(8,128)(2,1)}, f32[64,128]{1,0:T(8,128)}, f32[64,128]{1,0:T(8,128)}) custom-call(f32[8,64,128]{2,1,0:T(8,128)} %get-tuple-element.15.own_ref, bf16[8,64,128]{2,1,0:T(8,128)(2,1)} %copy-done.5, s32[1,128]{1,0:T(1,128)} %bitcast.8), custom_call_target="tpu_custom_call" | custom-call | flops 1000000000 | bytes 1000000 | tf_op jit(solution)/shard_map/key_value_finish/pallas_call | solution.py:492
  19.1 2.8 %collective-permute-start.2 = (bf16[1,528,128]{2,1,0:T(8,128)(2,1)}, bf16[1,528,128]{2,1,0:T(8,128)(2,1)S(1)}, u32[]{:S(2)}, u32[]{:S(2)}) collective-permute-start(bf16[1,528,128]{2,1,0:T(8,128)(2,1)} %get-tuple-element.19), channel_id=1, source_target_pairs={{0,16},{2,18},{4,20},{6,22},{8,24},{10,26},{12,28},{14,30},{16,0},... | collective-permute-start | bytes 405512 | tf_op jit(solution)/shard_map/ppermute | solution.py:431
  21.9 6.0 %collective-permute-done.2 = bf16[1,528,128]{2,1,0:T(8,128)(2,1)S(1)} collective-permute-done((bf16[1,528,128]{2,1,0:T(8,128)(2,1)}, bf16[1,528,128]{2,1,0:T(8,128)(2,1)S(1)}, u32[]{:S(2)}, u32[]{:S(2)}) %collective-permute-start.2) | collective-permute-done | bytes 135200 | tf_op jit(solution)/shard_map/ppermute | solution.py:431
  27.9 0.9 pad_maximum_fusion
  28.8 0.8 collective-permute-start.3
  29.6 0.9 constant_dynamic-update-slice_fusion.2
  30.5 5.8 %collective-permute-done.3 = bf16[2,528,128]{2,1,0:T(8,128)(2,1)S(1)} collective-permute-done((bf16[2,528,128]{2,1,0:T(8,128)(2,1)S(1)}, bf16[2,528,128]{2,1,0:T(8,128)(2,1)S(1)}, u32[]{:S(2)}, u32[]{:S(2)}) %collective-permute-start.3) | collective-permute-done | bytes 270368 | tf_op jit(solution)/shard_map/ppermute | solution.py:431
  36.4 1.4 %collective-permute-start.4 = (bf16[4,528,128]{2,1,0:T(8,128)(2,1)S(1)}, bf16[4,528,128]{2,1,0:T(8,128)(2,1)S(1)}, u32[]{:S(2)}, u32[]{:S(2)}) collective-permute-start(bf16[4,528,128]{2,1,0:T(8,128)(2,1)S(1)} %constant_dynamic-update-slice_fusion.own_ref), channel_id=1, source_target_pairs={{0,4},{2,6},{4,0},{6,2},{8,12},{10,14},{12,8},{14,10},{16,20},{18,... | collective-permute-start | bytes 1622024 | tf_op jit(solution)/shard_map/ppermute | solution.py:431
  37.8 8.8 %query_send.1 = bf16[8,128,128]{2,1,0:T(8,128)(2,1)} custom-call(bf16[128,4096]{1,0:T(8,128)(2,1)} %get-tuple-element.13.x_ref.normed_ref, s32[2048,384]{1,0:T(8,128)} %codes_ref.3, s32[32,3072]{1,0:T(8,128)} %scale_ref.5, f32[1,64]{1,0:T(1,128)} %bitcast.10), custom_call_target="tpu_custom_call" | custom-call | flops 12000000000 | bytes 1048576 | tf_op jit(solution)/shard_map/query_send/pallas_call | solution.py:481
  46.6 1.5 %collective-permute-start = (bf16[8,128,128]{2,1,0:T(8,128)(2,1)}, bf16[8,128,128]{2,1,0:T(8,128)(2,1)S(1)}, u32[]{:S(2)}, u32[]{:S(2)}) collective-permute-start(bf16[8,128,128]{2,1,0:T(8,128)(2,1)} %query_send.1), channel_id=1, source_target_pairs={{0,1},{1,0},{2,3},{3,2},{4,5},{5,4},{6,7},{7,6},{8,9},{9,8},{10,11... | collective-permute-start | bytes 786440 | tf_op jit(solution)/shard_map/ppermute | solution.py:434
  48.9 9.1 %query_own.1.own_ref = f32[8,128,128]{2,1,0:T(8,128)} custom-call(bf16[128,4096]{1,0:T(8,128)(2,1)} %get-tuple-element.13.x_ref.normed_ref, s32[2048,384]{1,0:T(8,128)} %codes_ref.3, s32[32,3072]{1,0:T(8,128)} %scale_ref.5, f32[1,64]{1,0:T(1,128)} %bitcast.11), custom_call_target="tpu_custom_call" | custom-call | flops 12000000000 | bytes 1048576 | tf_op jit(solution)/shard_map/query_own/pallas_call | solution.py:481
  58.7 2.6 %query_finish.1.queries_ref = bf16[8,128,128]{2,1,0:T(8,128)(2,1)} custom-call(f32[8,128,128]{2,1,0:T(8,128)} %query_own.1.own_ref, bf16[8,128,128]{2,1,0:T(8,128)(2,1)} %copy-done.4, bf16[128,16]{1,0:T(8,128)(2,1)} %get-tuple-element.14.low_rank_ref, bf16[16,1024]{1,0:T(8,128)(2,1)} %up_ref.3, f32[64,128]{1,0:T(8,128)} %get-tuple-element.17.cosine_ref, ...), custom_call_target="tpu_custom_call" | custom-call | flops 2000000000 | bytes 1000000 | tf_op jit(solution)/shard_map/query_finish/pallas_call | solution.py:506
  61.3 0.8 copy-done.2
  62.1 0.8 copy-done.3
  62.9 7.5 %attention.1 = (bf16[128,1024]{1,0:T(8,128)(2,1)}, f32[16,2560]{1,0:T(8,128)}, bf16[16,2560]{1,0:T(8,128)(2,1)}) custom-call(bf16[8,128,128]{2,1,0:T(8,128)(2,1)} %query_finish.1.queries_ref, bf16[128,1024]{1,0:T(8,128)(2,1)} %cotangent_ref.1, bf16[4,528,128]{2,1,0:T(8,128)(2,1)} %copy-done, bf16[4,528,128]{2,1,0:T(8,128)(2,1)} %copy-done.1, ...), custom_call_target="tpu_custom_call" | custom-call | flops 10000000000 | bytes 1000000 | tf_op jit(solution)/shard_map/attention/pallas_call | solution.py:527
  70.7 1.2 %collective-permute-done.7 = bf16[16,2560]{1,0:T(8,128)(2,1)S(1)} collective-permute-done((bf16[16,2560]{1,0:T(8,128)(2,1)}, bf16[16,2560]{1,0:T(8,128)(2,1)S(1)}, u32[]{:S(2)}, u32[]{:S(2)}) %collective-permute-start.7) | collective-permute-done | bytes 81952 | tf_op jit(solution)/shard_map/ppermute | solution.py:431
  71.9 0.9 fusion
  72.8 1.4 %collective-permute-start.8 = (bf16[16,2560]{1,0:T(8,128)(2,1)S(1)}, bf16[16,2560]{1,0:T(8,128)(2,1)S(1)}, u32[]{:S(2)}, u32[]{:S(2)}) collective-permute-start(bf16[16,2560]{1,0:T(8,128)(2,1)S(1)} %fusion), channel_id=1, source_target_pairs={{0,4},{2,6},{4,0},{6,2},{8,12},{10,14},{12,8},{14,10},{16,20},{18,... | collective-permute-start | bytes 245768 | tf_op jit(solution)/shard_map/ppermute | solution.py:431
  74.2 3.4 %collective-permute-done.8 = bf16[16,2560]{1,0:T(8,128)(2,1)S(1)} collective-permute-done((bf16[16,2560]{1,0:T(8,128)(2,1)S(1)}, bf16[16,2560]{1,0:T(8,128)(2,1)S(1)}, u32[]{:S(2)}, u32[]{:S(2)}) %collective-permute-start.8) | collective-permute-done | bytes 81952 | tf_op jit(solution)/shard_map/ppermute | solution.py:431
  77.6 1.0 fusion.2
  78.5 4.4 %collective-permute-start.9 = (bf16[16,2560]{1,0:T(8,128)(2,1)S(1)}, bf16[16,2560]{1,0:T(8,128)(2,1)S(1)}, u32[]{:S(2)}, u32[]{:S(2)}) collective-permute-start(bf16[16,2560]{1,0:T(8,128)(2,1)S(1)} %fusion.2), channel_id=1, source_target_pairs={{0,8},{2,10},{4,12},{6,14},{8,0},{10,2},{12,4},{14,6},{16,24},{18,... | collective-permute-start | bytes 245768 | tf_op jit(solution)/shard_map/ppermute | solution.py:431
  82.9 2.4 %collective-permute-done.9 = bf16[16,2560]{1,0:T(8,128)(2,1)S(1)} collective-permute-done((bf16[16,2560]{1,0:T(8,128)(2,1)S(1)}, bf16[16,2560]{1,0:T(8,128)(2,1)S(1)}, u32[]{:S(2)}, u32[]{:S(2)}) %collective-permute-start.9) | collective-permute-done | bytes 81952 | tf_op jit(solution)/shard_map/ppermute | solution.py:431
  85.4 1.0 fusion.1
  86.3 8.6 %collective-permute-start.10 = (bf16[16,2560]{1,0:T(8,128)(2,1)S(1)}, bf16[16,2560]{1,0:T(8,128)(2,1)S(1)}, u32[]{:S(2)}, u32[]{:S(2)}) collective-permute-start(bf16[16,2560]{1,0:T(8,128)(2,1)S(1)} %fusion.1), channel_id=1, source_target_pairs={{0,16},{2,18},{4,20},{6,22},{8,24},{10,26},{12,28},{14,30},{16,0},... | collective-permute-start | bytes 245768 | tf_op jit(solution)/shard_map/ppermute | solution.py:431
  94.9 2.4 %collective-permute-done.10 = bf16[16,2560]{1,0:T(8,128)(2,1)S(1)} collective-permute-done((bf16[16,2560]{1,0:T(8,128)(2,1)S(1)}, bf16[16,2560]{1,0:T(8,128)(2,1)S(1)}, u32[]{:S(2)}, u32[]{:S(2)}) %collective-permute-start.10) | collective-permute-done | bytes 81952 | tf_op jit(solution)/shard_map/ppermute | solution.py:431
  97.3 1.0 convert_add_fusion
  98.3 1.4 %collective-permute-start.11 = (bf16[16,2048]{1,0:T(8,128)(2,1)S(1)}, bf16[16,2048]{1,0:T(8,128)(2,1)S(1)}, u32[]{:S(2)}, u32[]{:S(2)}) collective-permute-start(bf16[16,2048]{1,0:T(8,128)(2,1)S(1)} %slice.32), channel_id=1, source_target_pairs={{0,1},{1,0},{2,3},{3,2},{4,5},{5,4},{6,7},{7,6},{8,9},{9,8},{10,11... | collective-permute-start | bytes 196616 | tf_op jit(solution)/shard_map/ppermute | solution.py:434
  99.7 3.0 %collective-permute-done.11 = bf16[16,2048]{1,0:T(8,128)(2,1)S(1)} collective-permute-done((bf16[16,2048]{1,0:T(8,128)(2,1)S(1)}, bf16[16,2048]{1,0:T(8,128)(2,1)S(1)}, u32[]{:S(2)}, u32[]{:S(2)}) %collective-permute-start.11) | collective-permute-done | bytes 65568 | tf_op jit(solution)/shard_map/ppermute | solution.py:434
  102.8 1.4 %collective-permute-done.12 = f32[16,2560]{1,0:T(8,128)S(1)} collective-permute-done((f32[16,2560]{1,0:T(8,128)S(1)}, f32[16,2560]{1,0:T(8,128)S(1)}, u32[]{:S(2)}, u32[]{:S(2)}) %collective-permute-start.12) | collective-permute-done | bytes 163872 | tf_op jit(solution)/shard_map/ppermute | solution.py:431
  (31 shorter events, 4.0 us)
Async XLA Ops:
  9.8 6.7 %collective-permute-start.1 = (bf16[8,64,128]{2,1,0:T(8,128)(2,1)}, bf16[8,64,128]{2,1,0:T(8,128)(2,1)S(1)}, u32[]{:S(2)}, u32[]{:S(2)}) collective-permute-start(bf16[8,64,128]{2,1,0:T(8,128)(2,1)} %get-tuple-element.16), channel_id=1, source_target_pairs={{0,1},{1,0},{2,3},{3,2},{4,5},{5,4},{6,7},{7,6},{8,9},{9,8},{10,11... | collective-permute-start | bytes 393224 | tf_op jit(solution)/shard_map/ppermute | solution.py:434
  16.5 0.7 copy-start.5
  19.1 8.8 %collective-permute-start.2 = (bf16[1,528,128]{2,1,0:T(8,128)(2,1)}, bf16[1,528,128]{2,1,0:T(8,128)(2,1)S(1)}, u32[]{:S(2)}, u32[]{:S(2)}) collective-permute-start(bf16[1,528,128]{2,1,0:T(8,128)(2,1)} %get-tuple-element.19), channel_id=1, source_target_pairs={{0,16},{2,18},{4,20},{6,22},{8,24},{10,26},{12,28},{14,30},{16,0},... | collective-permute-start | bytes 405512 | tf_op jit(solution)/shard_map/ppermute | solution.py:431
  28.8 7.5 %collective-permute-start.3 = (bf16[2,528,128]{2,1,0:T(8,128)(2,1)S(1)}, bf16[2,528,128]{2,1,0:T(8,128)(2,1)S(1)}, u32[]{:S(2)}, u32[]{:S(2)}) collective-permute-start(bf16[2,528,128]{2,1,0:T(8,128)(2,1)S(1)} %pad_maximum_fusion), channel_id=1, source_target_pairs={{0,8},{2,10},{4,12},{6,14},{8,0},{10,2},{12,4},{14,6},{16,24},{18,... | collective-permute-start | bytes 811016 | tf_op jit(solution)/shard_map/ppermute | solution.py:431
  36.4 11.7 %copy-start = (bf16[4,528,128]{2,1,0:T(8,128)(2,1)}, bf16[4,528,128]{2,1,0:T(8,128)(2,1)S(1)}, u32[]{:S(2)}) copy-start(bf16[4,528,128]{2,1,0:T(8,128)(2,1)S(1)} %constant_dynamic-update-slice_fusion.own_ref) | copy-start | bytes 1622020
  36.4 12.5 %collective-permute-start.4 = (bf16[4,528,128]{2,1,0:T(8,128)(2,1)S(1)}, bf16[4,528,128]{2,1,0:T(8,128)(2,1)S(1)}, u32[]{:S(2)}, u32[]{:S(2)}) collective-permute-start(bf16[4,528,128]{2,1,0:T(8,128)(2,1)S(1)} %constant_dynamic-update-slice_fusion.own_ref), channel_id=1, source_target_pairs={{0,4},{2,6},{4,0},{6,2},{8,12},{10,14},{12,8},{14,10},{16,20},{18,... | collective-permute-start | bytes 1622024 | tf_op jit(solution)/shard_map/ppermute | solution.py:431
  46.6 11.4 %collective-permute-start = (bf16[8,128,128]{2,1,0:T(8,128)(2,1)}, bf16[8,128,128]{2,1,0:T(8,128)(2,1)S(1)}, u32[]{:S(2)}, u32[]{:S(2)}) collective-permute-start(bf16[8,128,128]{2,1,0:T(8,128)(2,1)} %query_send.1), channel_id=1, source_target_pairs={{0,1},{1,0},{2,3},{3,2},{4,5},{5,4},{6,7},{7,6},{8,9},{9,8},{10,11... | collective-permute-start | bytes 786440 | tf_op jit(solution)/shard_map/ppermute | solution.py:434
  48.1 13.1 %collective-permute-start.5 = (bf16[4,528,128]{2,1,0:T(8,128)(2,1)S(1)}, bf16[4,528,128]{2,1,0:T(8,128)(2,1)S(1)}, u32[]{:S(2)}, u32[]{:S(2)}) collective-permute-start(bf16[4,528,128]{2,1,0:T(8,128)(2,1)S(1)} %constant_dynamic-update-slice_fusion.own_ref), channel_id=1, source_target_pairs={{0,2},{2,0},{4,6},{6,4},{8,10},{10,8},{12,14},{14,12},{16,18},{18,... | collective-permute-start | bytes 1622024 | tf_op jit(solution)/shard_map/ppermute | solution.py:431
  48.9 9.1 %copy-start.1 = (bf16[4,528,128]{2,1,0:T(8,128)(2,1)}, bf16[4,528,128]{2,1,0:T(8,128)(2,1)S(1)}, u32[]{:S(2)}) copy-start(bf16[4,528,128]{2,1,0:T(8,128)(2,1)S(1)} %collective-permute-done.4.beside_ref) | copy-start | bytes 1622020
  48.9 12.4 %collective-permute-start.6 = (bf16[4,528,128]{2,1,0:T(8,128)(2,1)S(1)}, bf16[4,528,128]{2,1,0:T(8,128)(2,1)S(1)}, u32[]{:S(2)}, u32[]{:S(2)}) collective-permute-start(bf16[4,528,128]{2,1,0:T(8,128)(2,1)S(1)} %collective-permute-done.4.beside_ref), channel_id=1, source_target_pairs={{0,2},{2,0},{4,6},{6,4},{8,10},{10,8},{12,14},{14,12},{16,18},{18,... | collective-permute-start | bytes 1622024 | tf_op jit(solution)/shard_map/ppermute | solution.py:431
  58.0 0.7 copy-start.4
  61.3 0.8 copy-start.2
  62.1 0.8 copy-start.3
  70.4 1.5 %collective-permute-start.7 = (bf16[16,2560]{1,0:T(8,128)(2,1)}, bf16[16,2560]{1,0:T(8,128)(2,1)S(1)}, u32[]{:S(2)}, u32[]{:S(2)}) collective-permute-start(bf16[16,2560]{1,0:T(8,128)(2,1)} %get-tuple-element.22), channel_id=1, source_target_pairs={{0,2},{2,0},{4,6},{6,4},{8,10},{10,8},{12,14},{14,12},{16,18},{18,... | collective-permute-start | bytes 245768 | tf_op jit(solution)/shard_map/ppermute | solution.py:431
  72.8 4.7 %collective-permute-start.8 = (bf16[16,2560]{1,0:T(8,128)(2,1)S(1)}, bf16[16,2560]{1,0:T(8,128)(2,1)S(1)}, u32[]{:S(2)}, u32[]{:S(2)}) collective-permute-start(bf16[16,2560]{1,0:T(8,128)(2,1)S(1)} %fusion), channel_id=1, source_target_pairs={{0,4},{2,6},{4,0},{6,2},{8,12},{10,14},{12,8},{14,10},{16,20},{18,... | collective-permute-start | bytes 245768 | tf_op jit(solution)/shard_map/ppermute | solution.py:431
  78.5 6.8 %collective-permute-start.9 = (bf16[16,2560]{1,0:T(8,128)(2,1)S(1)}, bf16[16,2560]{1,0:T(8,128)(2,1)S(1)}, u32[]{:S(2)}, u32[]{:S(2)}) collective-permute-start(bf16[16,2560]{1,0:T(8,128)(2,1)S(1)} %fusion.2), channel_id=1, source_target_pairs={{0,8},{2,10},{4,12},{6,14},{8,0},{10,2},{12,4},{14,6},{16,24},{18,... | collective-permute-start | bytes 245768 | tf_op jit(solution)/shard_map/ppermute | solution.py:431
  86.3 11.0 %collective-permute-start.10 = (bf16[16,2560]{1,0:T(8,128)(2,1)S(1)}, bf16[16,2560]{1,0:T(8,128)(2,1)S(1)}, u32[]{:S(2)}, u32[]{:S(2)}) collective-permute-start(bf16[16,2560]{1,0:T(8,128)(2,1)S(1)} %fusion.1), channel_id=1, source_target_pairs={{0,16},{2,18},{4,20},{6,22},{8,24},{10,26},{12,28},{14,30},{16,0},... | collective-permute-start | bytes 245768 | tf_op jit(solution)/shard_map/ppermute | solution.py:431
  98.3 4.3 %collective-permute-start.11 = (bf16[16,2048]{1,0:T(8,128)(2,1)S(1)}, bf16[16,2048]{1,0:T(8,128)(2,1)S(1)}, u32[]{:S(2)}, u32[]{:S(2)}) collective-permute-start(bf16[16,2048]{1,0:T(8,128)(2,1)S(1)} %slice.32), channel_id=1, source_target_pairs={{0,1},{1,0},{2,3},{3,2},{4,5},{5,4},{6,7},{7,6},{8,9},{9,8},{10,11... | collective-permute-start | bytes 196616 | tf_op jit(solution)/shard_map/ppermute | solution.py:434
  102.7 1.5 %collective-permute-start.12 = (f32[16,2560]{1,0:T(8,128)S(1)}, f32[16,2560]{1,0:T(8,128)S(1)}, u32[]{:S(2)}, u32[]{:S(2)}) collective-permute-start(f32[16,2560]{1,0:T(8,128)S(1)} %pad_maximum_fusion.1), channel_id=1, source_target_pairs={{0,2},{2,0},{4,6},{6,4},{8,10},{10,8},{12,14},{14,12},{16,18},{18,... | collective-permute-start | bytes 491528 | tf_op jit(solution)/shard_map/ppermute | solution.py:431

commit v2 on v1

--- a/solution.py
+++ b/solution.py
@@ -13,6 +13,8 @@
 NIBBLES = 8
 GROUP = HEAD_SIZE // NIBBLES
 DEPTH = 256
+STRIP = 16
+TOP_BITS = [8 << (4 * n) for n in range(7)] + [-(1 << 31)]
 
 NF4_LEVELS = [
     -1.0,
@@ -32,6 +34,8 @@
     0.7229568362236023,
     1.0,
 ]
+LIMIT = pltpu.CompilerParams(vmem_limit_bytes=16 * 2**20)
+WIDE_LIMIT = pltpu.CompilerParams(vmem_limit_bytes=40 * 2**20)
 ADAPTER_SCALE = 2.0
 ROPE_BASE = 500000.0
 F32 = jnp.float32
@@ -81,42 +85,68 @@
         out_ref[n] = column.T
 
 
-def project(words, x_ref, x_start, scales_ref, weight_ref, total_ref, row_count):
+def code_words_copies(codes_ref, lane_start, buffer_ref, sems_ref):
+    steps = buffer_ref.shape[0]
+    return [
+        pltpu.make_async_copy(
+            codes_ref.at[pl.ds(step * DEPTH, DEPTH), pl.ds(lane_start, 2 * HEAD_SIZE)],
+            buffer_ref.at[step],
+            sems_ref.at[step],
+        )
+        for step in range(steps)
+    ]
+
+
+def pick(table, index):
+    numbers = lax.GatherDimensionNumbers(
+        offset_dims=(),
+        collapsed_slice_dims=(0,),
+        start_index_map=(0,),
+        operand_batching_dims=(1,),
+        start_indices_batching_dims=(1,),
+    )
+    mode = lax.GatherScatterMode.PROMISE_IN_BOUNDS
+    return lax.gather(table, index[..., None], numbers, slice_sizes=(1, 1), mode=mode)
+
+
+def table_rows(levels):
+    place = lax.broadcasted_iota(jnp.int32, (8, HEAD_SIZE), 0)
+    table = jnp.zeros((8, HEAD_SIZE), F32)
+    for index, level in enumerate(levels):
+        table = jnp.where(place == index, F32(level), table)
+    return table
+
+
+def project(words, wait, x_ref, x_start, scales_ref, weight_ref, total_ref, row_count):
     steps = row_count // DEPTH
+    tables = (table_rows(NF4_LEVELS[:8]), table_rows(NF4_LEVELS[8:]))
 
     def fill(step, slot):
+        wait(step)
         for part in range(DEPTH // BLOCK_ROWS):
-            start = pl.multiple_of(step * DEPTH + part * BLOCK_ROWS, BLOCK_ROWS)
-            word = words(start)
+            word = words(step, part)
             block = step * (DEPTH // BLOCK_ROWS) + part
-            for half in range(2):
-                code = (lax.shift_right_logical(word, 16) if half else word).astype(jnp.int16)
-                for quarter in range(4):
-                    n = half * 4 + quarter
-                    bits = []
-                    for b in range(4):
-                        place = 4 * quarter + b
-                        if place == 15:
-                            bits.append(code < jnp.int16(0))
-                        else:
-                            bits.append((code & jnp.int16(1 << place)) != jnp.int16(0))
-                    level = [
-                        jnp.where(bits[3], BF16(NF4_LEVELS[8 + j]), BF16(NF4_LEVELS[j]))
-                        for j in range(8)
-                    ]
-                    level = [jnp.where(bits[2], level[4 + j], level[j]) for j in range(4)]
-                    level = [jnp.where(bits[1], level[2 + j], level[j]) for j in range(2)]
-                    level = jnp.where(bits[0], level[1], level[0])
-                    scale = scales_ref[n, pl.ds(block, 1), :].astype(BF16)
-                    weight_ref[
-                        slot,
-                        part * BLOCK_ROWS : (part + 1) * BLOCK_ROWS,
-                        n * HEAD_SIZE : (n + 1) * HEAD_SIZE,
-                    ] = level * scale
+            rows = slice(part * BLOCK_ROWS, (part + 1) * BLOCK_ROWS)
+            for n in range(NIBBLES):
+                scale = scales_ref[n, pl.ds(block, 1), :]
+                index = (lax.shift_right_logical(word, 4 * n) if n else word) & 7
+                upper = (word & jnp.int32(TOP_BITS[n])) != 0
+                pieces = []
+                for k in range(0, BLOCK_ROWS, 8):
+                    low, high = (pick(table, index[k : k + 8]) for table in tables)
+                    pieces.append(jnp.where(upper[k : k + 8], high, low) * scale)
+                weight = jnp.concatenate(pieces, axis=0).astype(BF16)
+                weight_ref[slot, n, rows, :] = weight
 
     def multiply(step, slot):
         start = pl.multiple_of(x_start + step * DEPTH, DEPTH)
-        total_ref[...] += nn(x_ref[:, pl.ds(start, DEPTH)], weight_ref[slot])
+        left = x_ref[:, pl.ds(start, DEPTH)]
+        for pair in range(NIBBLES // 2):
+            right = jnp.concatenate(
+                [weight_ref[slot, 2 * pair], weight_ref[slot, 2 * pair + 1]], axis=1
+            )
+            columns = slice(2 * pair * HEAD_SIZE, 2 * (pair + 1) * HEAD_SIZE)
+            total_ref[:, columns] += nn(left, right)
 
     total_ref[...] = jnp.zeros_like(total_ref)
     fill(0, 0)
@@ -133,35 +163,46 @@
 def key_value_kernel(
     x_ref,
     gain_ref,
-    low_codes_ref,
-    high_codes_ref,
+    codes_ref,
     scale_ref,
     second_ref,
-    down_ref,
     normed_ref,
-    low_rank_ref,
     own_ref,
     send_ref,
     scales_ref,
     weight_ref,
     total_ref,
     turned_ref,
+    words_ref,
+    sems_ref,
 ):
     member = lax.axis_index("fsdp")
-    row_count = low_codes_ref.shape[0]
+    row_count = codes_ref.shape[0]
+    copies = code_words_copies(codes_ref, HEAD_SIZE, words_ref, sems_ref)
+    for copy in copies:
+        copy.start()
     wide = x_ref[...].astype(F32)
     inverse = lax.rsqrt(jnp.mean(wide * wide, axis=-1, keepdims=True) + 1e-05)
     normed_ref[...] = (wide * inverse * gain_ref[...]).astype(BF16)
-    low_rank_ref[...] = nt(normed_ref[...], down_ref[...]).astype(BF16)
     spread_scales(scale_ref, second_ref, member, [8, 9, 10, 11, 20, 21, 22, 23], scales_ref)
     lane = lax.broadcasted_iota(jnp.int32, (BLOCK_ROWS, HEAD_SIZE), 1)
 
-    def words(start):
-        low = low_codes_ref[pl.ds(start, BLOCK_ROWS), :]
-        high = high_codes_ref[pl.ds(start, BLOCK_ROWS), :]
+    def words(step, part):
+        rows = slice(part * BLOCK_ROWS, (part + 1) * BLOCK_ROWS)
+        low = words_ref[step, rows, :HEAD_SIZE]
+        high = words_ref[step, rows, HEAD_SIZE:]
         return jnp.where(lane < HEAD_SIZE // 2, low, high)
 
-    project(words, normed_ref, member * row_count, scales_ref, weight_ref, total_ref, row_count)
+    def wait(step):
+        pltpu.make_async_copy(
+            codes_ref.at[pl.ds(0, DEPTH), pl.ds(HEAD_SIZE, 2 * HEAD_SIZE)],
+            words_ref.at[step],
+            sems_ref.at[step],
+        ).wait()
+
+    project(
+        words, wait, normed_ref, member * row_count, scales_ref, weight_ref, total_ref, row_count
+    )
     half = HEAD_SIZE // 2
     for n in range(NIBBLES):
         turned_ref[...] = total_ref[:, n * HEAD_SIZE : (n + 1) * HEAD_SIZE].T
@@ -172,7 +213,7 @@
 
 def query_kernel(
     first,
-    x_ref,
+    normed_hbm_ref,
     codes_ref,
     scale_ref,
     second_ref,
@@ -180,25 +221,47 @@
     scales_ref,
     weight_ref,
     total_ref,
+    words_ref,
+    sems_ref,
+    x_ref,
+    x_sem,
 ):
     member = lax.axis_index("fsdp")
     target = (1 - member) if first else member
     row_count = codes_ref.shape[0]
+    lane_start = pl.multiple_of(target * HEAD_SIZE, HEAD_SIZE)
+    fetch = pltpu.make_async_copy(
+        normed_hbm_ref.at[:, pl.ds(pl.multiple_of(member * row_count, HEAD_SIZE), row_count)],
+        x_ref,
+        x_sem,
+    )
+    copies = code_words_copies(codes_ref, lane_start, words_ref, sems_ref)
+    copies[0].start()
+    fetch.start()
+    for copy in copies[1:]:
+        copy.start()
     tiles = [
         jnp.where(target == 0, k, (16 + k) if k < 4 else (8 + k)) for k in range(NIBBLES)
     ]
     spread_scales(scale_ref, second_ref, member, tiles, scales_ref)
     lane = lax.broadcasted_iota(jnp.int32, (BLOCK_ROWS, HEAD_SIZE), 1)
-    is_low = target == 0
-
-    def words(start):
-        rows = pl.ds(start, BLOCK_ROWS)
-        zero = codes_ref[rows, :HEAD_SIZE]
-        low = codes_ref[rows, HEAD_SIZE : 2 * HEAD_SIZE]
-        high = codes_ref[rows, 2 * HEAD_SIZE :]
-        return jnp.where(is_low, zero, jnp.where(lane < HEAD_SIZE // 2, high, low))
-
-    project(words, x_ref, member * row_count, scales_ref, weight_ref, total_ref, row_count)
+    take_high = (lane < HEAD_SIZE // 2) & (target == 1)
+
+    def words(step, part):
+        rows = slice(part * BLOCK_ROWS, (part + 1) * BLOCK_ROWS)
+        low = words_ref[step, rows, :HEAD_SIZE]
+        high = words_ref[step, rows, HEAD_SIZE:]
+        return jnp.where(take_high, high, low)
+
+    def wait(step):
+        pltpu.make_async_copy(
+            codes_ref.at[pl.ds(0, DEPTH), pl.ds(0, 2 * HEAD_SIZE)],
+            words_ref.at[step],
+            sems_ref.at[step],
+        ).wait()
+
+    fetch.wait()
+    project(words, wait, x_ref, 0, scales_ref, weight_ref, total_ref, row_count)
     for n in range(NIBBLES):
         out_ref[n] = total_ref[:, n * HEAD_SIZE : (n + 1) * HEAD_SIZE].T.astype(out_ref.dtype)
 
@@ -240,9 +303,19 @@
 
 
 def query_finish_kernel(
-    own_ref, got_ref, low_rank_ref, up_ref, cosine_ref, sine_ref, queries_ref, full_ref
+    own_ref,
+    got_ref,
+    normed_ref,
+    down_ref,
+    up_ref,
+    cosine_ref,
+    sine_ref,
+    queries_ref,
+    low_rank_ref,
+    full_ref,
 ):
     member = lax.axis_index("fsdp")
+    low_rank_ref[...] = nt(normed_ref[...], down_ref[...]).astype(BF16)
     order = feature_permutation()
     heads = queries_ref.shape[0]
     for n in range(NIBBLES):
@@ -263,106 +336,136 @@
         queries_ref[head] = jnp.concatenate(pieces, axis=0).T.astype(BF16)
 
 
-def attention_kernel(
-    context,
-    queries_ref,
-    cotangent_ref,
-    own_ref,
-    beside_ref,
-    core_ref,
-    core_beside_ref,
-    low_rank_ref,
-    normed_ref,
-    up_ref,
-    cosine_ref,
-    sine_ref,
-    attn_ref,
-    mine_ref,
-    other_ref,
-    grads_ref,
-    top_ref,
-    norm_ref,
-    dot_ref,
-    out_ref,
-    grad_ref,
-    lin_ref,
-):
+def attention_kernel(context, flips, first, *refs):
+    queries_ref, cotangent_ref = refs[:2]
+    pieces = refs[2:4]
+    if first:
+        ids_ref = pieces[0]
+        state = refs[4:9]
+        before = None
+        bias_ref, scores_ref, dots_ref, expo_ref = refs[9:13]
+    else:
+        ids_ref = refs[4]
+        before = refs[5:10]
+        low_rank_ref, normed_ref, up_ref, cosine_ref, sine_ref = refs[10:15]
+        attn_ref, mine_ref, other_ref = refs[15:18]
+        state = refs[18:23]
+        bias_ref, scores_ref, dots_ref, expo_ref, lin_ref = refs[23:28]
+    top_ref, norm_ref, dot_ref, out_ref, grad_ref = state
     place = lax.axis_index("ctx")
     heads, row_count, _ = queries_ref.shape
     grouped = heads // 2
-    lists = own_ref.shape[0]
+    stack = grouped * row_count
+    lists = pieces[0].shape[0]
+    taken = min(lists, 4)
+    span = taken * len(pieces) * row_count
     depth = context.bit_length() - 1
     soft = math.log2(math.e) / math.sqrt(HEAD_SIZE)
-    for head in range(heads):
-        rows = slice((head % grouped) * row_count, (head % grouped + 1) * row_count)
-        grads_ref[head // grouped, rows, :] = cotangent_ref[
-            :, head * HEAD_SIZE : (head + 1) * HEAD_SIZE
-        ]
-    top_ref[...] = jnp.full_like(top_ref, -1e30)
-    norm_ref[...] = jnp.zeros_like(norm_ref)
-    dot_ref[...] = jnp.zeros_like(dot_ref)
-    out_ref[...] = jnp.zeros_like(out_ref)
-    grad_ref[...] = jnp.zeros_like(grad_ref)
     square = (row_count, row_count)
-    my_ids = own_ref[0, 4 * row_count :, :].astype(F32)[:1]
+    my_ids = ids_ref[0, 4 * row_count :, :].astype(F32)[:1]
     row_ids = jnp.broadcast_to(my_ids, square).T
     row_pos = lax.broadcasted_iota(jnp.int32, square, 0) + place * row_count
     lane = lax.broadcasted_iota(jnp.int32, square, 1)
-    pieces = (own_ref, beside_ref, core_ref, core_beside_ref)
-
-    def chunk(number, device):
-        bias = []
-        for piece, flip in zip(pieces, (0, 2, 1, 3)):
+
+    def device_of(number):
+        flip = 0
+        for b in range(depth - 2):
+            flip = flip + (((number >> b) & 1) << (depth - 1 - b))
+        return place ^ flip
+
+    def lowest(step):
+        highest = depth - 3 - (taken.bit_length() - 1)
+        kept = device_of(step * taken) & ~(context - 1 - ((1 << (highest + 3)) - 1))
+        return kept & ~3
+
+    def chunk(start, source):
+        numbers = [start + k for k in range(taken)]
+        blocks = [(piece, number) for piece in pieces for number in numbers]
+        for index, (piece, number) in enumerate(blocks):
+            device = device_of(number) ^ flips[index // taken]
             ids = piece[number, 4 * row_count :, :].astype(F32)[:1]
-            pos = lane + (device ^ flip) * row_count
+            pos = lane + device * row_count
             allowed = (row_ids == ids) & (pos <= row_pos)
-            bias.append(jnp.where(allowed, 0.0, -1e30))
-        bias = jnp.concatenate(bias, axis=1)
+            bias_ref[:, index * row_count : (index + 1) * row_count] = jnp.where(
+                allowed, 0.0, -1e30
+            )
         for kv in range(2):
             key_rows = slice(kv * row_count, (kv + 1) * row_count)
             value_rows = slice((2 + kv) * row_count, (3 + kv) * row_count)
-            keys = jnp.concatenate([piece[number, key_rows, :] for piece in pieces], axis=0)
-            values = jnp.concatenate([piece[number, value_rows, :] for piece in pieces], axis=0)
-            both = jnp.concatenate([values, keys], axis=1)
-            for g in range(grouped):
-                rows = slice(g * row_count, (g + 1) * row_count)
-                scores = nt(queries_ref[kv * grouped + g], keys) * soft + bias
-                dots = nt(grads_ref[kv, rows, :], values)
-                old = top_ref[kv, rows, :]
-                new = jnp.maximum(old, jnp.max(scores, axis=1, keepdims=True))
+            keys = jnp.concatenate([p[k, key_rows, :] for p, k in blocks], axis=0)
+            values = jnp.concatenate([p[k, value_rows, :] for p, k in blocks], axis=0)
+            query = queries_ref[kv * grouped : (kv + 1) * grouped].reshape(stack, HEAD_SIZE)
+            grads = jnp.concatenate(
+                [
+                    cotangent_ref[:, (kv * grouped + g) * HEAD_SIZE : (kv * grouped + g + 1) * HEAD_SIZE]
+                    for g in range(grouped)
+                ],
+                axis=0,
+            )
+            scores_ref[kv] = nt(query, keys)
+            dots_ref[kv] = nt(grads, values)
+        for kv in range(2):
+            key_rows = slice(kv * row_count, (kv + 1) * row_count)
+            value_rows = slice((2 + kv) * row_count, (3 + kv) * row_count)
+            decays = []
+            for strip in range(stack // STRIP):
+                rows = slice(strip * STRIP, (strip + 1) * STRIP)
+                at = strip * STRIP % row_count
+                scores = scores_ref[kv, rows, :] * soft + bias_ref[at : at + STRIP, :]
+                new = jnp.max(scores, axis=1, keepdims=True)
+                if source is not None:
+                    old = source[0][kv, rows, :]
+                    new = jnp.maximum(old, new)
+                    decay = jnp.exp2(old - new)
+                    decays.append(decay)
+                else:
+                    new = jnp.broadcast_to(new, (STRIP, HEAD_SIZE))
+                wide = jnp.concatenate([new] * (span // HEAD_SIZE), axis=1)
+                expo = jnp.exp2(scores - wide)
+                weighted = expo * dots_ref[kv, rows, :]
+                norm = fold(expo)
+                dot = fold(weighted)
+                if source is not None:
+                    norm = norm + decay * source[1][kv, rows, :]
+                    dot = dot + decay * source[2][kv, rows, :]
                 top_ref[kv, rows, :] = new
-                decay = jnp.exp2(old - new)
-                expo = jnp.exp2(scores - jnp.concatenate([new] * 4, axis=1))
-                weighted = expo * dots
-                fold = lambda a: (
-                    a[:, :HEAD_SIZE]
-                    + a[:, HEAD_SIZE : 2 * HEAD_SIZE]
-                    + a[:, 2 * HEAD_SIZE : 3 * HEAD_SIZE]
-                    + a[:, 3 * HEAD_SIZE :]
+                norm_ref[kv, rows, :] = norm
+                dot_ref[kv, rows, :] = dot
+                expo_ref[kv, rows, :] = expo.astype(BF16)
+                expo_ref[kv, stack + strip * STRIP : stack + (strip + 1) * STRIP, :] = (
+                    weighted.astype(BF16)
                 )
-                norm_ref[kv, rows, :] = decay * norm_ref[kv, rows, :] + fold(expo)
-                dot_ref[kv, rows, :] = decay * dot_ref[kv, rows, :] + fold(weighted)
-                wide = jnp.concatenate([decay, decay], axis=1)
-                out_ref[kv, rows, :] = wide * out_ref[kv, rows, :] + nn(expo.astype(BF16), both)
-                grad_ref[kv, rows, :] = decay * grad_ref[kv, rows, :] + nn(
-                    weighted.astype(BF16), keys
-                )
-
-    def body(number, carry):
-        flip = 0
-        for b in range(depth - 2):
-            flip = flip + (((number >> b) & 1) << (depth - 1 - b))
-        device = place ^ flip
-
-        @pl.when((device >> 2) <= (place >> 2))
-        def _():
-            chunk(number, device)
-
-        return carry
-
-    lax.fori_loop(0, lists, body, 0)
-
-    half = HEAD_SIZE // 2
+            both = jnp.concatenate(
+                [
+                    jnp.concatenate([p[k, value_rows, :], p[k, key_rows, :]], axis=1)
+                    for p, k in blocks
+                ],
+                axis=0,
+            )
+            product = nn(expo_ref[kv, :stack, :], both)
+            graded = nn(expo_ref[kv, stack:, :], both[:, HEAD_SIZE:])
+            if source is not None:
+                decay = jnp.concatenate(decays, axis=0)
+                product = product + jnp.concatenate([decay, decay], axis=1) * source[3][kv]
+                graded = graded + decay * source[4][kv]
+            out_ref[kv] = product
+            grad_ref[kv] = graded
+
+    chunk(0, before)
+    if lists > taken:
+
+        def body(step, carry):
+
+            @pl.when(lowest(step) <= place)
+            def _():
+                chunk(step * taken, state)
+
+            return carry
+
+        lax.fori_loop(1, lists // taken, body, 0)
+    if first:
+        return
+
     cosine, sine = [], []
     for n in range(NIBBLES):
         rows = slice(n * NIBBLES, (n + 1) * NIBBLES)
@@ -403,6 +506,13 @@
     other_ref[:, width:] = (ADAPTER_SCALE * tn(low_rank_ref[...], lin_ref[:, other])).astype(BF16)
 
 
+def fold(a):
+    total = a[:, :HEAD_SIZE]
+    for start in range(HEAD_SIZE, a.shape[1], HEAD_SIZE):
+        total = total + a[:, start : start + HEAD_SIZE]
+    return total
+
+
 def cost(flops, size):
     return pl.CostEstimate(flops=int(flops), bytes_accessed=int(size), transcendentals=0)
 
@@ -437,58 +547,51 @@
     second_row = block_second_scale.reshape(1, -1)
     ids_row = token_document.reshape(1, row_count)
     down_rows = query_down_map.T
+    steps = code_rows // DEPTH
     project_scratch = [
         pltpu.VMEM((NIBBLES, code_rows // BLOCK_ROWS, HEAD_SIZE), F32),
-        pltpu.VMEM((2, DEPTH, NIBBLES * HEAD_SIZE), BF16),
+        pltpu.VMEM((2, NIBBLES, DEPTH, HEAD_SIZE), BF16),
         pltpu.VMEM((row_count, NIBBLES * HEAD_SIZE), F32),
     ]
+    words_scratch = [
+        pltpu.VMEM((steps, DEPTH, 2 * HEAD_SIZE), jnp.int32),
+        pltpu.SemaphoreType.DMA((steps,)),
+    ]
     project_cost = cost(1.2e10, code_rows * HEAD_SIZE * 4)
-    whole = lambda a: pl.BlockSpec(a.shape, lambda i: (0,) * a.ndim)
-    normed, low_rank, kv_own, kv_send = pl.pallas_call(
+    anywhere = pl.BlockSpec(memory_space=pl.ANY)
+    normed, kv_own, kv_send = pl.pallas_call(
         key_value_kernel,
-        grid=(1,),
-        in_specs=[
-            whole(layer_input),
-            whole(gain_row),
-            pl.BlockSpec((code_rows, HEAD_SIZE), lambda i: (0, 1)),
-            pl.BlockSpec((code_rows, HEAD_SIZE), lambda i: (0, 2)),
-            whole(column_scale_quantized),
-            whole(second_row),
-            whole(down_rows),
-        ],
-        out_specs=vmem(4),
+        in_specs=vmem(2) + [anywhere] + vmem(2),
+        out_specs=vmem(3),
         out_shape=[
             sds((row_count, width), BF16),
-            sds((row_count, rank), BF16),
             sds((NIBBLES, half, row_count), F32),
             sds((NIBBLES, half, row_count), BF16),
         ],
-        scratch_shapes=project_scratch + [pltpu.VMEM((HEAD_SIZE, row_count), F32)],
+        scratch_shapes=project_scratch + [pltpu.VMEM((HEAD_SIZE, row_count), F32)] + words_scratch,
         cost_estimate=project_cost,
+        compiler_params=LIMIT,
         name="key_value_projection",
-    )(
-        layer_input,
-        gain_row,
-        codes,
-        codes,
-        column_scale_quantized,
-        second_row,
-        down_rows,
-    )
+    )(layer_input, gain_row, codes, column_scale_quantized, second_row)
     kv_got = swap(kv_send)
 
     def query_projection(first, dtype):
         return pl.pallas_call(
             functools.partial(query_kernel, first),
-            in_specs=vmem(4),
+            in_specs=[anywhere] * 2 + vmem(2),
             out_specs=pl.BlockSpec(memory_space=pltpu.VMEM),
             out_shape=sds((NIBBLES, HEAD_SIZE, row_count), dtype),
-            scratch_shapes=project_scratch,
+            scratch_shapes=project_scratch
+            + words_scratch
+            + [pltpu.VMEM((row_count, code_rows), BF16), pltpu.SemaphoreType.DMA],
             cost_estimate=project_cost,
-            name="query_send" if first else "query_own",
+            compiler_params=LIMIT,
+        name="query_send" if first else "query_own",
         )(normed, codes, column_scale_quantized, second_row)
 
     q_send = query_projection(True, BF16)
+    q_got = swap(q_send)
+    kv_got, q_send = lax.optimization_barrier((kv_got, q_send))
     block, cosine, sine = pl.pallas_call(
         key_value_finish_kernel,
         in_specs=vmem(3),
@@ -499,58 +602,77 @@
             sds((half, row_count), F32),
         ],
         cost_estimate=cost(1e9, 1e6),
+        compiler_params=LIMIT,
         name="key_value_finish",
     )(kv_own, kv_got, ids_row)
-    q_got = swap(q_send)
     q_own = query_projection(False, F32)
-    queries = pl.pallas_call(
+    queries, low_rank = pl.pallas_call(
         query_finish_kernel,
-        in_specs=vmem(6),
-        out_specs=pl.BlockSpec(memory_space=pltpu.VMEM),
-        out_shape=sds((heads, row_count, HEAD_SIZE), BF16),
+        in_specs=vmem(7),
+        out_specs=vmem(2),
+        out_shape=[sds((heads, row_count, HEAD_SIZE), BF16), sds((row_count, rank), BF16)],
         scratch_shapes=[pltpu.VMEM((NIBBLES, HEAD_SIZE, row_count), F32)],
         cost_estimate=cost(2e9, 1e6),
+        compiler_params=LIMIT,
         name="query_finish",
-    )(q_own, q_got, low_rank, query_up_map, cosine, sine)
+    )(q_own, q_got, normed, down_rows, query_up_map, cosine, sine)
 
     bit = context // 2
+    beside_work = [q_own, queries]
     while bit > 2:
-        block = jnp.concatenate([block, flip(block, bit)], axis=0)
+        got = flip(block, bit)
+        if beside_work:
+            got, _ = lax.optimization_barrier((got, beside_work.pop(0)))
+        block = jnp.concatenate([block, got], axis=0)
         bit //= 2
     beside = flip(block, 2)
     core = flip(block, 1)
+
+    lists = block.shape[0]
+    span = min(lists, 4) * 2 * row_count
+    stack = heads // 2 * row_count
+    state_shapes = [(2, stack, HEAD_SIZE)] * 3 + [(2, stack, 2 * HEAD_SIZE), (2, stack, HEAD_SIZE)]
+    work_shapes = [
+        pltpu.VMEM((row_count, span), F32),
+        pltpu.VMEM((2, stack, span), F32),
+        pltpu.VMEM((2, stack, span), F32),
+        pltpu.VMEM((2, 2 * stack, span), BF16),
+    ]
+    state = pl.pallas_call(
+        functools.partial(attention_kernel, context, (0, 1), True),
+        in_specs=vmem(4),
+        out_specs=vmem(5),
+        out_shape=[sds(shape, F32) for shape in state_shapes],
+        scratch_shapes=work_shapes,
+        cost_estimate=cost(8e9, 1e6),
+        compiler_params=WIDE_LIMIT,
+        name="attention_near",
+    )(queries, output_cotangent, block, core)
+    beside, state = lax.optimization_barrier((beside, tuple(state)))
     core_beside = flip(beside, 1)
-
     total = width // 2 + query_width // 2
-    stacked = (2, heads // 2 * row_count, HEAD_SIZE)
-    doubled = (2, heads // 2 * row_count, 2 * HEAD_SIZE)
     attn, mine, other = pl.pallas_call(
-        functools.partial(attention_kernel, context),
-        in_specs=vmem(11),
+        functools.partial(attention_kernel, context, (2, 3), False),
+        in_specs=vmem(15),
         out_specs=vmem(3),
         out_shape=[
             sds((row_count, query_width), BF16),
             sds((rank, total), F32),
             sds((rank, total), BF16),
         ],
-        scratch_shapes=[
-            pltpu.VMEM(stacked, BF16),
-            pltpu.VMEM(stacked, F32),
-            pltpu.VMEM(stacked, F32),
-            pltpu.VMEM(stacked, F32),
-            pltpu.VMEM(doubled, F32),
-            pltpu.VMEM(stacked, F32),
-            pltpu.VMEM((row_count, query_width), BF16),
-        ],
+        scratch_shapes=[pltpu.VMEM(shape, F32) for shape in state_shapes]
+        + work_shapes
+        + [pltpu.VMEM((row_count, query_width), BF16)],
         cost_estimate=cost(1e10, 1e6),
-        name="attention",
+        compiler_params=WIDE_LIMIT,
+        name="attention_far",
     )(
         queries,
         output_cotangent,
+        beside,
+        core_beside,
         block,
-        beside,
-        core,
-        core_beside,
+        *state,
         low_rank,
         normed,
         query_up_map,

time: 106 us -> 81.4 us (0.77)
  Pallas kernels: 39.1 us -> 25.8 us
  starting transfers between devices: 25.7 us -> 17.8 us
  other arithmetic: 6.16 us -> 1.59 us
  local copies, waits for them, and re-layouts: 3.97 us -> 5.62 us
    pallas_call x5 -> x6, Pallas kernels: 37.1 us -> 25.5 us  [the longest x2 10.9 us: query_projection(): pl.pallas_call(functools.partial(query_kernel, first), in_specs=[anywhere...]
    ppermute x10, starting transfers between devices: 19.8 us -> 13.1 us  [flip(): return lax.ppermute(array, 'ctx', [(i, i ^ bit) for i in range(context)])]
    ppermute x3, waiting for transfers between devices: 6.68 us -> 2.76 us  [swap(): return lax.ppermute(array, 'fsdp', [(0, 1), (1, 0)])]
    ppermute x10, waiting for transfers between devices: 23.3 us -> 26.7 us  [flip(): return lax.ppermute(array, 'ctx', [(i, i ^ bit) for i in range(context)])]
    convert_element_type x3, other arithmetic: 2.85 us -> 0.1 us  [on_device(): summed = summed + flip(summed.astype(BF16), bit).astype(F32)]
    pallas_call x1, Pallas kernels: 1.96 us -> 0.27 us  [on_device(): pl.pallas_call(key_value_finish_kernel, in_specs=vmem(3), out_specs=vmem(...]
    unnamed x14 -> x26, local copies, waits for them, and re-layouts: 3.9 us -> 5.54 us
    ppermute x3, starting transfers between devices: 5.87 us -> 4.75 us  [swap(): return lax.ppermute(array, 'fsdp', [(0, 1), (1, 0)])]
  transfers between devices with their start and end apart: 13 -> 13, of which waited for: 10 -> 11; matrix products, arithmetic and copies ran while one was open for 1% -> 0% of each run, Pallas kernels for 19% -> 20%
where the time goes in v2:
time: 81.4 us; the launch traced here: 81.1 us
  waiting for transfers between devices  29.5 us (36%)
  Pallas kernels  25.8 us (32%)
  starting transfers between devices  17.8 us (22%)
  local copies, waits for them, and re-layouts  5.62 us (7%)
  other arithmetic  1.59 us (2%)
  between operations  0.84 us (1%)
    ppermute x10, waiting for transfers between devices, flip(): return lax.ppermute(array, 'ctx', [(i, i ^ bit) for i in range(context)])  26.7 us
    ppermute x10, starting transfers between devices, flip(): return lax.ppermute(array, 'ctx', [(i, i ^ bit) for i in range(context)])  13.1 us
    pallas_call x2, Pallas kernels, query_projection(): pl.pallas_call(functools.partial(query_kernel, first), in_specs=[anywhere...  10.9 us
    pallas_call x1, Pallas kernels, on_device(): pl.pallas_call(key_value_kernel, in_specs=vmem(2) + [anywhere] + vmem(2),...  5.55 us
    unnamed x26, local copies, waits for them, and re-layouts  5.54 us
    ppermute x3, starting transfers between devices, swap(): return lax.ppermute(array, 'fsdp', [(0, 1), (1, 0)])  4.75 us
    pallas_call x1, Pallas kernels, on_device(): pl.pallas_call(functools.partial(attention_kernel, context, (2, 3), False...  3.86 us
    pallas_call x1, Pallas kernels, on_device(): pl.pallas_call(functools.partial(attention_kernel, context, (0, 1), True)...  2.87 us
  transfers between devices with their start and end apart: 13, of which 11 were waited for; matrix products, arithmetic and copies ran while one was open for 0% of the time, Pallas kernels for 20%

profile of v2, /device:TPU:0, one launch (start us, length us, event | category | flops | bytes accessed | tf_op | source)
XLA Modules:
  0.0 81.1 jit_solution(11852829724128734007)
XLA Ops:
  0.6 1.9 %copy-done = s32[2048,384]{1,0:T(8,128)S(1)} copy-done((s32[2048,384]{1,0:T(8,128)S(1)}, s32[2048,384]{1,0:T(8,128)}, u32[]{:S(2)}) %copy-start) | copy-done | bytes 3145752
  2.5 1.2 %copy-done.2 = bf16[128,4096]{1,0:T(8,128)(2,1)S(1)} copy-done((bf16[128,4096]{1,0:T(8,128)(2,1)S(1)}, bf16[128,4096]{1,0:T(8,128)(2,1)}, u32[]{:S(2)}) %copy-start.2) | copy-done | bytes 1048600
  3.7 1.0 %copy-done.3 = s32[32,3072]{1,0:T(8,128)S(1)} copy-done((s32[32,3072]{1,0:T(8,128)S(1)}, s32[32,3072]{1,0:T(8,128)}, u32[]{:S(2)}) %copy-start.3) | copy-done | bytes 393240
  4.7 0.7 copy-done.8
  5.5 0.7 copy-done.10
  6.1 5.5 %key_value_projection.1 = (bf16[128,4096]{1,0:T(8,128)(2,1)S(1)}, f32[8,64,128]{2,1,0:T(8,128)S(1)}, bf16[8,64,128]{2,1,0:T(8,128)(2,1)S(1)}) custom-call(bf16[128,4096]{1,0:T(8,128)(2,1)S(1)} %copy-done.2, f32[1,4096]{1,0:T(1,128)S(1)} %bitcast.7, s32[2048,384]{1,0:T(8,128)S(1)} %copy-done, s32[32,3072]{1,0:T(8,128)S(1)} %copy-done.3, f32[1,64]{1,0:T(1,128)S(1)} %bitcast.9), custom_call_target="tpu_custom_call" | custom-call | flops 12000000000 | bytes 1048576 | tf_op jit(solution)/shard_map/key_value_projection/pallas_call | solution.py:562
  11.7 3.1 %collective-permute-start.1 = (bf16[8,64,128]{2,1,0:T(8,128)(2,1)S(1)}, bf16[8,64,128]{2,1,0:T(8,128)(2,1)S(1)}, u32[]{:S(2)}, u32[]{:S(2)}) collective-permute-start(bf16[8,64,128]{2,1,0:T(8,128)(2,1)S(1)} %get-tuple-element.30), channel_id=1, source_target_pairs={{0,1},{1,0},{2,3},{3,2},{4,5},{5,4},{6,7},{7,6},{8,9},{9,8},{10,11... | collective-permute-start | bytes 393224 | tf_op jit(solution)/shard_map/ppermute | solution.py:544
  14.8 5.3 %query_send.1 = bf16[8,128,128]{2,1,0:T(8,128)(2,1)S(1)} custom-call(bf16[128,4096]{1,0:T(8,128)(2,1)S(1)} %get-tuple-element.28.normed_hbm_ref.normed_ref.refs_11_, s32[2048,384]{1,0:T(8,128)S(1)} %copy-done.1, s32[32,3072]{1,0:T(8,128)S(1)} %copy-done.4, f32[1,64]{1,0:T(1,128)S(1)} %bitcast.10), custom_call_target="tpu_custom_call" | custom-call | flops 12000000000 | bytes 1048576 | tf_op jit(solution)/shard_map/query_send/pallas_call | solution.py:579
  20.2 0.3 key_value_finish.1
  20.5 3.1 %collective-permute-start.2 = (bf16[1,528,128]{2,1,0:T(8,128)(2,1)S(1)}, bf16[1,528,128]{2,1,0:T(8,128)(2,1)S(1)}, u32[]{:S(2)}, u32[]{:S(2)}) collective-permute-start(bf16[1,528,128]{2,1,0:T(8,128)(2,1)S(1)} %get-tuple-element.35), channel_id=1, source_target_pairs={{0,16},{2,18},{4,20},{6,22},{8,24},{10,26},{12,28},{14,30},{16,0},... | collective-permute-start | bytes 405512 | tf_op jit(solution)/shard_map/ppermute | solution.py:541
  23.6 5.6 %query_own.1.own_ref = f32[8,128,128]{2,1,0:T(8,128)S(1)} custom-call(bf16[128,4096]{1,0:T(8,128)(2,1)S(1)} %get-tuple-element.28.normed_hbm_ref.normed_ref.refs_11_, s32[2048,384]{1,0:T(8,128)S(1)} %copy-done.1, s32[32,3072]{1,0:T(8,128)S(1)} %copy-done.4, f32[1,64]{1,0:T(1,128)S(1)} %bitcast.11), custom_call_target="tpu_custom_call" | custom-call | flops 12000000000 | bytes 1048576 | tf_op jit(solution)/shard_map/query_own/pallas_call | solution.py:579
  29.2 0.3 collective-permute-done.2
  29.6 1.3 %collective-permute-start.3 = (bf16[2,528,128]{2,1,0:T(8,128)(2,1)S(1)}, bf16[2,528,128]{2,1,0:T(8,128)(2,1)S(1)}, u32[]{:S(2)}, u32[]{:S(2)}) collective-permute-start(bf16[2,528,128]{2,1,0:T(8,128)(2,1)S(1)} %pad_maximum_fusion), channel_id=1, source_target_pairs={{0,8},{2,10},{4,12},{6,14},{8,0},{10,2},{12,4},{14,6},{16,24},{18,... | collective-permute-start | bytes 811016 | tf_op jit(solution)/shard_map/ppermute | solution.py:541
  30.9 2.4 %query_finish.1 = (bf16[8,128,128]{2,1,0:T(8,128)(2,1)S(1)}, bf16[128,16]{1,0:T(8,128)(2,1)S(1)}) custom-call(f32[8,128,128]{2,1,0:T(8,128)S(1)} %query_own.1.own_ref, bf16[8,128,128]{2,1,0:T(8,128)(2,1)S(1)} %collective-permute-done.got_ref, bf16[128,4096]{1,0:T(8,128)(2,1)S(1)} %get-tuple-element.28.normed_hbm_ref.normed_ref.refs_11_, ...), custom_call_target="tpu_custom_call" | custom-call | flops 2000000000 | bytes 1000000 | tf_op jit(solution)/shard_map/query_finish/pallas_call | solution.py:609
  33.3 3.7 %collective-permute-done.3 = bf16[2,528,128]{2,1,0:T(8,128)(2,1)S(1)} collective-permute-done((bf16[2,528,128]{2,1,0:T(8,128)(2,1)S(1)}, bf16[2,528,128]{2,1,0:T(8,128)(2,1)S(1)}, u32[]{:S(2)}, u32[]{:S(2)}) %collective-permute-start.3) | collective-permute-done | bytes 270368 | tf_op jit(solution)/shard_map/ppermute | solution.py:541
  37.1 1.7 %collective-permute-start.4 = (bf16[4,528,128]{2,1,0:T(8,128)(2,1)S(1)}, bf16[4,528,128]{2,1,0:T(8,128)(2,1)S(1)}, u32[]{:S(2)}, u32[]{:S(2)}) collective-permute-start(bf16[4,528,128]{2,1,0:T(8,128)(2,1)S(1)} %constant_dynamic-update-slice_fusion.refs_2_.refs_4_), channel_id=1, source_target_pairs={{0,4},{2,6},{4,0},{6,2},{8,12},{10,14},{12,8},{14,10},{16,20},{18,... | collective-permute-start | bytes 1622024 | tf_op jit(solution)/shard_map/ppermute | solution.py:541
  39.0 2.9 %attention_near.1 = (f32[2,512,128]{2,1,0:T(8,128)S(1)}, f32[2,512,128]{2,1,0:T(8,128)S(1)}, f32[2,512,128]{2,1,0:T(8,128)S(1)}, f32[2,512,256]{2,1,0:T(8,128)S(1)}, f32[2,512,128]{2,1,0:T(8,128)S(1)}) custom-call(bf16[8,128,128]{2,1,0:T(8,128)(2,1)S(1)} %get-tuple-element.34.refs_0_, bf16[128,1024]{1,0:T(8,128)(2,1)S(1)} %copy-done.5, ...), custom_call_target="tpu_custom_call" | custom-call | flops 8000000000 | bytes 1000000 | tf_op jit(solution)/shard_map/attention_near/pallas_call | solution.py:641
  41.9 9.9 %collective-permute-done.4.refs_2_ = bf16[4,528,128]{2,1,0:T(8,128)(2,1)S(1)} collective-permute-done((bf16[4,528,128]{2,1,0:T(8,128)(2,1)S(1)}, bf16[4,528,128]{2,1,0:T(8,128)(2,1)S(1)}, u32[]{:S(2)}, u32[]{:S(2)}) %collective-permute-start.4) | collective-permute-done | bytes 540704 | tf_op jit(solution)/shard_map/ppermute | solution.py:541
  51.8 1.9 %collective-permute-done.6.refs_3_ = bf16[4,528,128]{2,1,0:T(8,128)(2,1)S(1)} collective-permute-done((bf16[4,528,128]{2,1,0:T(8,128)(2,1)S(1)}, bf16[4,528,128]{2,1,0:T(8,128)(2,1)S(1)}, u32[]{:S(2)}, u32[]{:S(2)}) %collective-permute-start.6) | collective-permute-done | bytes 540704 | tf_op jit(solution)/shard_map/ppermute | solution.py:541
  53.7 3.9 %attention_far.1 = (bf16[128,1024]{1,0:T(8,128)(2,1)}, f32[16,2560]{1,0:T(8,128)S(1)}, bf16[16,2560]{1,0:T(8,128)(2,1)S(1)}) custom-call(bf16[8,128,128]{2,1,0:T(8,128)(2,1)S(1)} %get-tuple-element.34.refs_0_, bf16[128,1024]{1,0:T(8,128)(2,1)S(1)} %copy-done.5, bf16[4,528,128]{2,1,0:T(8,128)(2,1)S(1)} %collective-permute-done.4.refs_2_, ...), custom_call_target="tpu_custom_call" | custom-call | flops 10000000000 | bytes 1000000 | tf_op jit(solution)/shard_map/attention_far/pallas_call | solution.py:654
  57.7 1.1 %collective-permute-done.7 = bf16[16,2560]{1,0:T(8,128)(2,1)S(1)} collective-permute-done((bf16[16,2560]{1,0:T(8,128)(2,1)S(1)}, bf16[16,2560]{1,0:T(8,128)(2,1)S(1)}, u32[]{:S(2)}, u32[]{:S(2)}) %collective-permute-start.7) | collective-permute-done | bytes 81952 | tf_op jit(solution)/shard_map/ppermute | solution.py:541
  58.9 1.7 %collective-permute-start.8 = (bf16[16,2560]{1,0:T(8,128)(2,1)S(1)}, bf16[16,2560]{1,0:T(8,128)(2,1)S(1)}, u32[]{:S(2)}, u32[]{:S(2)}) collective-permute-start(bf16[16,2560]{1,0:T(8,128)(2,1)S(1)} %fusion), channel_id=1, source_target_pairs={{0,4},{2,6},{4,0},{6,2},{8,12},{10,14},{12,8},{14,10},{16,20},{18,... | collective-permute-start | bytes 245768 | tf_op jit(solution)/shard_map/ppermute | solution.py:541
  60.5 2.9 %collective-permute-done.8 = bf16[16,2560]{1,0:T(8,128)(2,1)S(1)} collective-permute-done((bf16[16,2560]{1,0:T(8,128)(2,1)S(1)}, bf16[16,2560]{1,0:T(8,128)(2,1)S(1)}, u32[]{:S(2)}, u32[]{:S(2)}) %collective-permute-start.8) | collective-permute-done | bytes 81952 | tf_op jit(solution)/shard_map/ppermute | solution.py:541
  63.5 1.7 %collective-permute-start.9 = (bf16[16,2560]{1,0:T(8,128)(2,1)S(1)}, bf16[16,2560]{1,0:T(8,128)(2,1)S(1)}, u32[]{:S(2)}, u32[]{:S(2)}) collective-permute-start(bf16[16,2560]{1,0:T(8,128)(2,1)S(1)} %fusion.2), channel_id=1, source_target_pairs={{0,8},{2,10},{4,12},{6,14},{8,0},{10,2},{12,4},{14,6},{16,24},{18,... | collective-permute-start | bytes 245768 | tf_op jit(solution)/shard_map/ppermute | solution.py:541
  65.2 2.8 %collective-permute-done.9 = bf16[16,2560]{1,0:T(8,128)(2,1)S(1)} collective-permute-done((bf16[16,2560]{1,0:T(8,128)(2,1)S(1)}, bf16[16,2560]{1,0:T(8,128)(2,1)S(1)}, u32[]{:S(2)}, u32[]{:S(2)}) %collective-permute-start.9) | collective-permute-done | bytes 81952 | tf_op jit(solution)/shard_map/ppermute | solution.py:541
  68.0 3.3 %collective-permute-start.10 = (bf16[16,2560]{1,0:T(8,128)(2,1)S(1)}, bf16[16,2560]{1,0:T(8,128)(2,1)S(1)}, u32[]{:S(2)}, u32[]{:S(2)}) collective-permute-start(bf16[16,2560]{1,0:T(8,128)(2,1)S(1)} %fusion.1), channel_id=1, source_target_pairs={{0,16},{2,18},{4,20},{6,22},{8,24},{10,26},{12,28},{14,30},{16,0},... | collective-permute-start | bytes 245768 | tf_op jit(solution)/shard_map/ppermute | solution.py:541
  71.4 2.4 %collective-permute-done.10 = bf16[16,2560]{1,0:T(8,128)(2,1)S(1)} collective-permute-done((bf16[16,2560]{1,0:T(8,128)(2,1)S(1)}, bf16[16,2560]{1,0:T(8,128)(2,1)S(1)}, u32[]{:S(2)}, u32[]{:S(2)}) %collective-permute-start.10) | collective-permute-done | bytes 81952 | tf_op jit(solution)/shard_map/ppermute | solution.py:541
  73.9 1.6 %collective-permute-start.11 = (bf16[16,2048]{1,0:T(8,128)(2,1)S(1)}, bf16[16,2048]{1,0:T(8,128)(2,1)S(1)}, u32[]{:S(2)}, u32[]{:S(2)}) collective-permute-start(bf16[16,2048]{1,0:T(8,128)(2,1)S(1)} %slice.32), channel_id=1, source_target_pairs={{0,1},{1,0},{2,3},{3,2},{4,5},{5,4},{6,7},{7,6},{8,9},{9,8},{10,11... | collective-permute-start | bytes 196616 | tf_op jit(solution)/shard_map/ppermute | solution.py:544
  75.4 2.8 %collective-permute-done.11 = bf16[16,2048]{1,0:T(8,128)(2,1)S(1)} collective-permute-done((bf16[16,2048]{1,0:T(8,128)(2,1)S(1)}, bf16[16,2048]{1,0:T(8,128)(2,1)S(1)}, u32[]{:S(2)}, u32[]{:S(2)}) %collective-permute-start.11) | collective-permute-done | bytes 65568 | tf_op jit(solution)/shard_map/ppermute | solution.py:544
  78.3 1.4 %collective-permute-done.12 = f32[16,2560]{1,0:T(8,128)S(1)} collective-permute-done((f32[16,2560]{1,0:T(8,128)S(1)}, f32[16,2560]{1,0:T(8,128)S(1)}, u32[]{:S(2)}, u32[]{:S(2)}) %collective-permute-start.12) | collective-permute-done | bytes 163872 | tf_op jit(solution)/shard_map/ppermute | solution.py:541
  79.8 0.6 pad_maximum_fusion.2
  80.4 0.7 maximum_bitcast_fusion
  (44 shorter events, 1.1 us)
Async XLA Ops:
  0.6 1.9 %copy-start = (s32[2048,384]{1,0:T(8,128)S(1)}, s32[2048,384]{1,0:T(8,128)}, u32[]{:S(2)}) copy-start(s32[2048,384]{1,0:T(8,128)} %codes_ref.5) | copy-start | bytes 9437188
  2.5 1.2 %copy-start.2 = (bf16[128,4096]{1,0:T(8,128)(2,1)S(1)}, bf16[128,4096]{1,0:T(8,128)(2,1)}, u32[]{:S(2)}) copy-start(bf16[128,4096]{1,0:T(8,128)(2,1)} %x_ref.1) | copy-start | bytes 3145732
  3.7 1.0 %copy-start.3 = (s32[32,3072]{1,0:T(8,128)S(1)}, s32[32,3072]{1,0:T(8,128)}, u32[]{:S(2)}) copy-start(s32[32,3072]{1,0:T(8,128)} %scale_ref.5) | copy-start | bytes 1179652
  4.7 0.7 copy-start.8
  5.5 0.7 copy-start.10
  6.1 8.6 %copy-start.1 = (s32[2048,384]{1,0:T(8,128)S(1)}, s32[2048,384]{1,0:T(8,128)}, u32[]{:S(2)}) copy-start(s32[2048,384]{1,0:T(8,128)} %codes_ref.5) | copy-start | bytes 9437188
  6.1 8.6 %copy-start.4 = (s32[32,3072]{1,0:T(8,128)S(1)}, s32[32,3072]{1,0:T(8,128)}, u32[]{:S(2)}) copy-start(s32[32,3072]{1,0:T(8,128)} %scale_ref.5) | copy-start | bytes 1179652
  11.7 8.5 %collective-permute-start.1 = (bf16[8,64,128]{2,1,0:T(8,128)(2,1)S(1)}, bf16[8,64,128]{2,1,0:T(8,128)(2,1)S(1)}, u32[]{:S(2)}, u32[]{:S(2)}) collective-permute-start(bf16[8,64,128]{2,1,0:T(8,128)(2,1)S(1)} %get-tuple-element.30), channel_id=1, source_target_pairs={{0,1},{1,0},{2,3},{3,2},{4,5},{5,4},{6,7},{7,6},{8,9},{9,8},{10,11... | collective-permute-start | bytes 393224 | tf_op jit(solution)/shard_map/ppermute | solution.py:544
  14.7 5.5 %copy-start.9 = (s32[128]{0:T(128)S(1)}, s32[128]{0:T(128)}, u32[]{:S(2)}) copy-start(s32[128]{0:T(128)} %param.16) | copy-start | bytes 1540
  20.1 3.5 %copy-start.11 = (f32[64]{0:T(128)S(1)}, f32[64]{0:T(128)}, u32[]{:S(2)}) copy-start(f32[64]{0:T(128)} %param.13) | copy-start | bytes 772
  20.1 10.8 %collective-permute-start = (bf16[8,128,128]{2,1,0:T(8,128)(2,1)S(1)}, bf16[8,128,128]{2,1,0:T(8,128)(2,1)S(1)}, u32[]{:S(2)}, u32[]{:S(2)}) collective-permute-start(bf16[8,128,128]{2,1,0:T(8,128)(2,1)S(1)} %query_send.1), channel_id=1, source_target_pairs={{0,1},{1,0},{2,3},{3,2},{4,5},{5,4},{6,7},{7,6},{8,9},{9,8},{10,11... | collective-permute-start | bytes 786440 | tf_op jit(solution)/shard_map/ppermute | solution.py:544
  20.5 10.4 %copy-start.6 = (bf16[4096,16]{0,1:T(8,128)(2,1)S(1)}, bf16[4096,16]{0,1:T(8,128)(2,1)}, u32[]{:S(2)}) copy-start(bf16[4096,16]{0,1:T(8,128)(2,1)} %param.14) | copy-start | bytes 393220
  20.5 10.4 %copy-start.7 = (bf16[16,1024]{1,0:T(8,128)(2,1)S(1)}, bf16[16,1024]{1,0:T(8,128)(2,1)}, u32[]{:S(2)}) copy-start(bf16[16,1024]{1,0:T(8,128)(2,1)} %refs_12_.1) | copy-start | bytes 98308
  20.5 9.0 %collective-permute-start.2 = (bf16[1,528,128]{2,1,0:T(8,128)(2,1)S(1)}, bf16[1,528,128]{2,1,0:T(8,128)(2,1)S(1)}, u32[]{:S(2)}, u32[]{:S(2)}) collective-permute-start(bf16[1,528,128]{2,1,0:T(8,128)(2,1)S(1)} %get-tuple-element.35), channel_id=1, source_target_pairs={{0,16},{2,18},{4,20},{6,22},{8,24},{10,26},{12,28},{14,30},{16,0},... | collective-permute-start | bytes 405512 | tf_op jit(solution)/shard_map/ppermute | solution.py:541
  29.6 7.4 %collective-permute-start.3 = (bf16[2,528,128]{2,1,0:T(8,128)(2,1)S(1)}, bf16[2,528,128]{2,1,0:T(8,128)(2,1)S(1)}, u32[]{:S(2)}, u32[]{:S(2)}) collective-permute-start(bf16[2,528,128]{2,1,0:T(8,128)(2,1)S(1)} %pad_maximum_fusion), channel_id=1, source_target_pairs={{0,8},{2,10},{4,12},{6,14},{8,0},{10,2},{12,4},{14,6},{16,24},{18,... | collective-permute-start | bytes 811016 | tf_op jit(solution)/shard_map/ppermute | solution.py:541
  30.9 8.1 %copy-start.5 = (bf16[128,1024]{1,0:T(8,128)(2,1)S(1)}, bf16[128,1024]{1,0:T(8,128)(2,1)}, u32[]{:S(2)}) copy-start(bf16[128,1024]{1,0:T(8,128)(2,1)} %refs_1_.3) | copy-start | bytes 786436
  37.0 2.0 %collective-permute-start.5 = (bf16[4,528,128]{2,1,0:T(8,128)(2,1)S(1)}, bf16[4,528,128]{2,1,0:T(8,128)(2,1)S(1)}, u32[]{:S(2)}, u32[]{:S(2)}) collective-permute-start(bf16[4,528,128]{2,1,0:T(8,128)(2,1)S(1)} %constant_dynamic-update-slice_fusion.refs_2_.refs_4_), channel_id=1, source_target_pairs={{0,2},{2,0},{4,6},{6,4},{8,10},{10,8},{12,14},{14,12},{16,18},{18,... | collective-permute-start | bytes 1622024 | tf_op jit(solution)/shard_map/ppermute | solution.py:541
  37.1 14.7 %collective-permute-start.4 = (bf16[4,528,128]{2,1,0:T(8,128)(2,1)S(1)}, bf16[4,528,128]{2,1,0:T(8,128)(2,1)S(1)}, u32[]{:S(2)}, u32[]{:S(2)}) collective-permute-start(bf16[4,528,128]{2,1,0:T(8,128)(2,1)S(1)} %constant_dynamic-update-slice_fusion.refs_2_.refs_4_), channel_id=1, source_target_pairs={{0,4},{2,6},{4,0},{6,2},{8,12},{10,14},{12,8},{14,10},{16,20},{18,... | collective-permute-start | bytes 1622024 | tf_op jit(solution)/shard_map/ppermute | solution.py:541
  51.8 1.9 %collective-permute-start.6 = (bf16[4,528,128]{2,1,0:T(8,128)(2,1)S(1)}, bf16[4,528,128]{2,1,0:T(8,128)(2,1)S(1)}, u32[]{:S(2)}, u32[]{:S(2)}) collective-permute-start(bf16[4,528,128]{2,1,0:T(8,128)(2,1)S(1)} %collective-permute-done.4.refs_2_), channel_id=1, source_target_pairs={{0,2},{2,0},{4,6},{6,4},{8,10},{10,8},{12,14},{14,12},{16,18},{18,... | collective-permute-start | bytes 1622024 | tf_op jit(solution)/shard_map/ppermute | solution.py:541
  57.6 1.3 %collective-permute-start.7 = (bf16[16,2560]{1,0:T(8,128)(2,1)S(1)}, bf16[16,2560]{1,0:T(8,128)(2,1)S(1)}, u32[]{:S(2)}, u32[]{:S(2)}) collective-permute-start(bf16[16,2560]{1,0:T(8,128)(2,1)S(1)} %get-tuple-element.52), channel_id=1, source_target_pairs={{0,2},{2,0},{4,6},{6,4},{8,10},{10,8},{12,14},{14,12},{16,18},{18,... | collective-permute-start | bytes 245768 | tf_op jit(solution)/shard_map/ppermute | solution.py:541
  58.9 4.6 %collective-permute-start.8 = (bf16[16,2560]{1,0:T(8,128)(2,1)S(1)}, bf16[16,2560]{1,0:T(8,128)(2,1)S(1)}, u32[]{:S(2)}, u32[]{:S(2)}) collective-permute-start(bf16[16,2560]{1,0:T(8,128)(2,1)S(1)} %fusion), channel_id=1, source_target_pairs={{0,4},{2,6},{4,0},{6,2},{8,12},{10,14},{12,8},{14,10},{16,20},{18,... | collective-permute-start | bytes 245768 | tf_op jit(solution)/shard_map/ppermute | solution.py:541
  63.5 4.5 %collective-permute-start.9 = (bf16[16,2560]{1,0:T(8,128)(2,1)S(1)}, bf16[16,2560]{1,0:T(8,128)(2,1)S(1)}, u32[]{:S(2)}, u32[]{:S(2)}) collective-permute-start(bf16[16,2560]{1,0:T(8,128)(2,1)S(1)} %fusion.2), channel_id=1, source_target_pairs={{0,8},{2,10},{4,12},{6,14},{8,0},{10,2},{12,4},{14,6},{16,24},{18,... | collective-permute-start | bytes 245768 | tf_op jit(solution)/shard_map/ppermute | solution.py:541
  68.0 5.8 %collective-permute-start.10 = (bf16[16,2560]{1,0:T(8,128)(2,1)S(1)}, bf16[16,2560]{1,0:T(8,128)(2,1)S(1)}, u32[]{:S(2)}, u32[]{:S(2)}) collective-permute-start(bf16[16,2560]{1,0:T(8,128)(2,1)S(1)} %fusion.1), channel_id=1, source_target_pairs={{0,16},{2,18},{4,20},{6,22},{8,24},{10,26},{12,28},{14,30},{16,0},... | collective-permute-start | bytes 245768 | tf_op jit(solution)/shard_map/ppermute | solution.py:541
  73.9 4.3 %collective-permute-start.11 = (bf16[16,2048]{1,0:T(8,128)(2,1)S(1)}, bf16[16,2048]{1,0:T(8,128)(2,1)S(1)}, u32[]{:S(2)}, u32[]{:S(2)}) collective-permute-start(bf16[16,2048]{1,0:T(8,128)(2,1)S(1)} %slice.32), channel_id=1, source_target_pairs={{0,1},{1,0},{2,3},{3,2},{4,5},{5,4},{6,7},{7,6},{8,9},{9,8},{10,11... | collective-permute-start | bytes 196616 | tf_op jit(solution)/shard_map/ppermute | solution.py:544
  78.2 1.5 %collective-permute-start.12 = (f32[16,2560]{1,0:T(8,128)S(1)}, f32[16,2560]{1,0:T(8,128)S(1)}, u32[]{:S(2)}, u32[]{:S(2)}) collective-permute-start(f32[16,2560]{1,0:T(8,128)S(1)} %pad_maximum_fusion.1), channel_id=1, source_target_pairs={{0,2},{2,0},{4,6},{6,4},{8,10},{10,8},{12,14},{14,12},{16,18},{18,... | collective-permute-start | bytes 491528 | tf_op jit(solution)/shard_map/ppermute | solution.py:541
